TPU v7x, 32 devices: a whole 2x2x4 slice. The times are simulated.
32 devices in a mesh: fsdp: 32 (over z, y, x, core).
Axes of the slice: x: 2, y: 2, z: 4, core: 2. Of those that a mesh axis runs over, the one named last changes fastest.
Arguments:
- tokens: int32 [1024, 2], P('fsdp')
- positions: int32 [1024], P('fsdp')
- src_len: int32 [1024], P('fsdp')
- self_k: bfloat16 [2, 1024, 32, 16, 64], P(None, 'fsdp')
- self_v: bfloat16 [2, 1024, 32, 16, 64], P(None, 'fsdp')
- cross_k: bfloat16 [2, 1024, 32, 16, 64], P(None, 'fsdp')
- cross_v: bfloat16 [2, 1024, 32, 16, 64], P(None, 'fsdp')
- attn_w: bfloat16 [2, 6, 1024, 1024], P(None, None, 'fsdp')
- attn_b: bfloat16 [2, 6, 1024], P(None, None, 'fsdp')
- fc1_w: bfloat16 [2, 1024, 4096], P(None, 'fsdp')
- fc1_b: bfloat16 [2, 4096], P(None, 'fsdp')
- fc2_w: bfloat16 [2, 4096, 1024], P(None, 'fsdp')
- fc2_b: bfloat16 [2, 1024], P(None, 'fsdp')
- ln_gain: bfloat16 [2, 3, 1024], P(None, None, 'fsdp')
- ln_bias: bfloat16 [2, 3, 1024], P(None, None, 'fsdp')
- tok_embed: bfloat16 [50304, 1024], P('fsdp')
- pos_embed: bfloat16 [1026, 1024], replicated
- emb_norm: bfloat16 [2, 1024], replicated
- logit_bias: float32 [50304], P('fsdp')
Outputs:
- output 1: float32 [2, 1024, 50304], P(None, None, 'fsdp')
- output 2: bfloat16 [2, 1024, 32, 16, 64], P(None, 'fsdp')
- output 3: bfloat16 [2, 1024, 32, 16, 64], P(None, 'fsdp')
All inputs are finite; a program needn't handle non-finite values.
Results may differ from a plain program's by a relative error of at most 0.00767352.
Values are sent between devices in bfloat16 or wider.
A program may use at most 1 GiB of HBM per device.

v0:
```python
import jax
import jax.numpy as jnp
from jax import lax
from jax.sharding import PartitionSpec as P, NamedSharding

LN_EPS = 1e-5


def layer_norm(values, gain_row, shift_row):
    row_mean = values.mean(-1, keepdims=True)
    centered = values - row_mean
    variance = (centered * centered).mean(-1, keepdims=True)
    return centered * lax.rsqrt(variance + LN_EPS) * gain_row.astype(jnp.float32) + shift_row.astype(jnp.float32)


def attend(query_rows, key_rows, val_rows, valid_len):
    scores = jnp.einsum('bhd,bthd->bht', query_rows, key_rows, preferred_element_type=jnp.float32)
    valid_mask = jnp.arange(key_rows.shape[1])[None, None, :] < valid_len[:, None, None]
    scores = jnp.where(valid_mask, scores, -jnp.inf)
    weights = jnp.exp(scores - scores.max(-1, keepdims=True))
    mixed_rows = jnp.einsum('bht,bthd->bhd', weights.astype(jnp.bfloat16), val_rows, preferred_element_type=jnp.float32)
    return mixed_rows / weights.sum(-1)[:, :, None]


def project(act_rows, weight, bias_row):
    return jnp.dot(act_rows, weight, preferred_element_type=jnp.float32) + bias_row.astype(jnp.float32)


def decoder_layer(hidden, step_pos, src_len, cache_k, cache_v, cross_k, cross_v, layer_w, layer_b, up_w, up_b, down_w, down_b, ln_gains, ln_shifts):
    num_rows, num_times, num_heads, head_dim = cache_k.shape
    attn_scale = head_dim ** -0.5
    act_rows = hidden.astype(jnp.bfloat16)
    qkv_rows = jnp.einsum('bd,sde->sbe', act_rows, layer_w[:3], preferred_element_type=jnp.float32) + layer_b[:3, None, :].astype(jnp.float32)
    self_query = (qkv_rows[0] * attn_scale).astype(jnp.bfloat16).reshape(num_rows, num_heads, head_dim)
    new_key = qkv_rows[1].astype(jnp.bfloat16).reshape(num_rows, 1, num_heads, head_dim)
    new_val = qkv_rows[2].astype(jnp.bfloat16).reshape(num_rows, 1, num_heads, head_dim)
    write_mask = (jnp.arange(num_times)[None, :] == step_pos[:, None])[:, :, None, None]
    cache_k = jnp.where(write_mask, new_key, cache_k)
    cache_v = jnp.where(write_mask, new_val, cache_v)
    mixed_rows = attend(self_query, cache_k, cache_v, step_pos + 1)
    attn_out = project(mixed_rows.reshape(num_rows, -1).astype(jnp.bfloat16), layer_w[3], layer_b[3])
    hidden = layer_norm(hidden + attn_out, ln_gains[0], ln_shifts[0])
    cross_query = (project(hidden.astype(jnp.bfloat16), layer_w[4], layer_b[4]) * attn_scale).astype(jnp.bfloat16).reshape(num_rows, num_heads, head_dim)
    mixed_rows = attend(cross_query, cross_k, cross_v, src_len)
    cross_out = project(mixed_rows.reshape(num_rows, -1).astype(jnp.bfloat16), layer_w[5], layer_b[5])
    hidden = layer_norm(hidden + cross_out, ln_gains[1], ln_shifts[1])
    inner_act = jax.nn.gelu(project(hidden.astype(jnp.bfloat16), up_w, up_b), approximate=False).astype(jnp.bfloat16)
    hidden = layer_norm(hidden + project(inner_act, down_w, down_b), ln_gains[2], ln_shifts[2])
    return hidden, cache_k, cache_v


def solution(mesh):
    cache_spec = P(None, 'fsdp')
    in_specs = (P('fsdp'), P('fsdp'), P('fsdp'), cache_spec, cache_spec, cache_spec, cache_spec,
                P(None, None, 'fsdp'), P(None, None, 'fsdp'), P(None, 'fsdp'), P(None, 'fsdp'),
                P(None, 'fsdp'), P(None, 'fsdp'), P(None, None, 'fsdp'), P(None, None, 'fsdp'),
                P('fsdp'), P(), P(), P('fsdp'))
    out_specs = (P(None, None, 'fsdp'), cache_spec, cache_spec)

    def local_decode(tokens, positions, src_len, self_k, self_v, cross_k, cross_v, attn_w, attn_b, fc1_w, fc1_b, fc2_w, fc2_b, ln_gain, ln_bias, tok_embed, pos_embed, emb_norm, logit_bias):
        shard_idx = lax.axis_index('fsdp')
        num_layers = attn_w.shape[0]
        num_steps = tokens.shape[1]
        vocab_local = tok_embed.shape[0]
        all_tokens = lax.all_gather(tokens, 'fsdp', axis=0, tiled=True)
        local_ids = all_tokens - shard_idx * vocab_local
        owned_mask = (local_ids >= 0) & (local_ids < vocab_local)
        picked = jnp.take(tok_embed, jnp.clip(local_ids, 0, vocab_local - 1), axis=0)
        picked = jnp.where(owned_mask[:, :, None], picked, jnp.zeros_like(picked))
        tok_rows = lax.psum_scatter(picked, 'fsdp', scatter_dimension=0, tiled=True)
        cache_k = [self_k[layer_idx] for layer_idx in range(num_layers)]
        cache_v = [self_v[layer_idx] for layer_idx in range(num_layers)]
        step_logits = []
        for step_idx in range(num_steps):
            step_pos = positions + step_idx
            start_rows = tok_rows[:, step_idx].astype(jnp.float32) + jnp.take(pos_embed, step_pos + 2, axis=0).astype(jnp.float32)
            hidden = layer_norm(start_rows, emb_norm[0], emb_norm[1])
            for layer_idx in range(num_layers):
                layer_w = lax.all_gather(attn_w[layer_idx], 'fsdp', axis=1, tiled=True)
                layer_b = lax.all_gather(attn_b[layer_idx], 'fsdp', axis=1, tiled=True)
                up_w = lax.all_gather(fc1_w[layer_idx], 'fsdp', axis=0, tiled=True)
                up_b = lax.all_gather(fc1_b[layer_idx], 'fsdp', axis=0, tiled=True)
                down_w = lax.all_gather(fc2_w[layer_idx], 'fsdp', axis=0, tiled=True)
                down_b = lax.all_gather(fc2_b[layer_idx], 'fsdp', axis=0, tiled=True)
                ln_gains = lax.all_gather(ln_gain[layer_idx], 'fsdp', axis=1, tiled=True)
                ln_shifts = lax.all_gather(ln_bias[layer_idx], 'fsdp', axis=1, tiled=True)
                hidden, cache_k[layer_idx], cache_v[layer_idx] = decoder_layer(
                    hidden, step_pos, src_len, cache_k[layer_idx], cache_v[layer_idx], cross_k[layer_idx], cross_v[layer_idx],
                    layer_w, layer_b, up_w, up_b, down_w, down_b, ln_gains, ln_shifts)
            all_rows = lax.all_gather(hidden.astype(jnp.bfloat16), 'fsdp', axis=0, tiled=True)
            logits = jnp.einsum('bd,vd->bv', all_rows, tok_embed, preferred_element_type=jnp.float32) + logit_bias
            step_logits.append(logits)
        return jnp.stack(step_logits), jnp.stack(cache_k), jnp.stack(cache_v)

    return jax.shard_map(local_decode, mesh=mesh, in_specs=in_specs, out_specs=out_specs, check_vma=False)
```

profile of v0, /device:TPU:0, one launch (start us, length us, event | category | flops | bytes accessed | tf_op | source)
XLA Modules:
  0.0 950.2 jit_solution(13790454538878503829)
XLA Ops:
  7.2 43.5 %all-gather.16 = s32[32,32,2]{1,2,0:T(2,128)S(1)} all-gather(s32[1,32,2]{1,2,0:T(2,128)} %bitcast.409), channel_id=1, replica_groups=mesh['fsdp'=32] {'fsdp'}, dimensions={0}, use_global_device_ids=true | all-gather | bytes 8448 | tf_op jit(solution)/shard_map/all_gather | solution.py:65
  53.3 9.6 %gather_fusion = bf16[2048,1024]{1,0:T(8,128)(2,1)} fusion(bf16[1572,1024]{1,0:T(8,128)(2,1)S(1)} %copy-done, s32[2048]{0:T(1024)S(1)} %broadcast_clamp_fusion), kind=kCustom, calls=%fused_computation.2 | custom fusion | bytes 8396800 | tf_op jit(solution)/shard_map/jit(_take)/gather | solution.py:68
  62.9 7.2 reshape.465
  70.2 6.0 fusion.56
  84.9 2.5 gather_fusion.1
  87.5 2.6 gather_fusion.2
  90.2 38.6 %all-gather.1 = bf16[1,6,1024]{1,0,2:T(2,128)(2,1)S(1)} all-gather(bf16[1,6,32]{1,0,2:T(2,128)(2,1)S(1)} %copy.125), channel_id=3, replica_groups=mesh['fsdp'=32] {'fsdp'}, dimensions={2}, use_global_device_ids=true | all-gather | bytes 12672 | tf_op jit(solution)/shard_map/all_gather | solution.py:80
  129.6 13.0 %fusion.186 = (f32[1024]{0:T(1024)}, f32[1024]{0:T(1024)}, f32[1024]{0:T(1024)}) fusion(bf16[1,6,1024]{1,0,2:T(2,128)(2,1)S(1)} %all-gather.1), kind=kLoop, calls=%fused_computation.213 | loop fusion | flops 3072 | bytes 18432 | tf_op jit(solution)/shard_map/add | solution.py:26
  144.7 39.6 %all-gather.2 = bf16[1,3,1024]{1,0,2:T(2,128)(2,1)S(1)} all-gather(bf16[1,3,32]{1,0,2:T(2,128)(2,1)S(1)} %copy.129), channel_id=4, replica_groups=mesh['fsdp'=32] {'fsdp'}, dimensions={2}, use_global_device_ids=true | all-gather | bytes 6336 | tf_op jit(solution)/shard_map/all_gather | solution.py:85
  184.3 11.1 %fusion.183 = (f32[1024]{0:T(1024)}, f32[1024]{0:T(1024)}, f32[1024]{0:T(1024)}) fusion(bf16[1,3,1024]{1,0,2:T(2,128)(2,1)S(1)} %all-gather.2), kind=kLoop, calls=%fused_computation.207 | loop fusion | flops 3072 | bytes 18432 | tf_op jit(solution)/shard_map/mul | solution.py:13
  195.6 40.3 %all-gather.3 = bf16[1,3,1024]{1,0,2:T(2,128)(2,1)S(1)} all-gather(bf16[1,3,32]{1,0,2:T(2,128)(2,1)S(1)} %copy.130), channel_id=5, replica_groups=mesh['fsdp'=32] {'fsdp'}, dimensions={2}, use_global_device_ids=true | all-gather | bytes 6336 | tf_op jit(solution)/shard_map/all_gather | solution.py:86
  235.8 11.1 %fusion.182 = (f32[1024]{0:T(1024)}, f32[1024]{0:T(1024)}, f32[1024]{0:T(1024)}) fusion(bf16[1,3,1024]{1,0,2:T(2,128)(2,1)S(1)} %all-gather.3), kind=kLoop, calls=%fused_computation.205 | loop fusion | flops 3072 | bytes 18432 | tf_op jit(solution)/shard_map/add | solution.py:13
  246.9 6.7 slice_bitcast_fusion.7
  254.3 4.3 slice_bitcast_fusion.8
  259.1 38.8 %all-reduce.2 = (bf16[1024]{0:T(1024)(128)(2,1)S(1)}, bf16[1024]{0:T(1024)(128)(2,1)S(1)}) all-reduce(bf16[1024]{0:T(1024)(128)(2,1)S(1)} %dynamic-update-slice, bf16[1024]{0:T(1024)(128)(2,1)S(1)} %dynamic-update-slice.1), channel_id=9, replica_groups=mesh['fsdp'=32] {'fsdp'}, use_global_device_ids=true, to_apply=%add | all-reduce | flops 2048 | bytes 8192
  298.5 40.0 %all-gather.5 = bf16[1,4096]{1,0:T(2,128)(2,1)S(1)} all-gather(bf16[1,128]{1,0:T(2,128)(2,1)S(1)} %get-tuple-element.120), channel_id=7, replica_groups=mesh['fsdp'=32] {'fsdp'}, dimensions={1}, use_global_device_ids=true | all-gather | bytes 8448 | tf_op jit(solution)/shard_map/all_gather | solution.py:82
  339.2 40.5 %all-gather.9 = bf16[1,6,1024]{1,0,2:T(2,128)(2,1)S(1)} all-gather(bf16[1,6,32]{1,0,2:T(2,128)(2,1)S(1)} %copy.127), channel_id=11, replica_groups=mesh['fsdp'=32] {'fsdp'}, dimensions={2}, use_global_device_ids=true | all-gather | bytes 12672 | tf_op jit(solution)/shard_map/all_gather | solution.py:80
  380.6 13.0 %fusion.177 = (f32[1024]{0:T(1024)}, f32[1024]{0:T(1024)}, f32[1024]{0:T(1024)}) fusion(bf16[1,6,1024]{1,0,2:T(2,128)(2,1)S(1)} %all-gather.9), kind=kLoop, calls=%fused_computation.195 | loop fusion | flops 3072 | bytes 18432 | tf_op jit(solution)/shard_map/add | solution.py:26
  396.3 39.3 %all-gather.10 = bf16[1,3,1024]{1,0,2:T(2,128)(2,1)S(1)} all-gather(bf16[1,3,32]{1,0,2:T(2,128)(2,1)S(1)} %copy.131), channel_id=12, replica_groups=mesh['fsdp'=32] {'fsdp'}, dimensions={2}, use_global_device_ids=true | all-gather | bytes 6336 | tf_op jit(solution)/shard_map/all_gather | solution.py:85
  435.7 11.1 %fusion.174 = (f32[1024]{0:T(1024)}, f32[1024]{0:T(1024)}, f32[1024]{0:T(1024)}) fusion(bf16[1,3,1024]{1,0,2:T(2,128)(2,1)S(1)} %all-gather.10), kind=kLoop, calls=%fused_computation.189 | loop fusion | flops 3072 | bytes 18432 | tf_op jit(solution)/shard_map/mul | solution.py:13
  446.9 40.3 %all-gather.11 = bf16[1,3,1024]{1,0,2:T(2,128)(2,1)S(1)} all-gather(bf16[1,3,32]{1,0,2:T(2,128)(2,1)S(1)} %copy.132), channel_id=13, replica_groups=mesh['fsdp'=32] {'fsdp'}, dimensions={2}, use_global_device_ids=true | all-gather | bytes 6336 | tf_op jit(solution)/shard_map/all_gather | solution.py:86
  487.2 11.1 %fusion.173 = (f32[1024]{0:T(1024)}, f32[1024]{0:T(1024)}, f32[1024]{0:T(1024)}) fusion(bf16[1,3,1024]{1,0,2:T(2,128)(2,1)S(1)} %all-gather.11), kind=kLoop, calls=%fused_computation.187 | loop fusion | flops 3072 | bytes 18432 | tf_op jit(solution)/shard_map/add | solution.py:13
  498.8 37.4 %all-gather.13 = bf16[1,4096]{1,0:T(2,128)(2,1)S(1)} all-gather(bf16[1,128]{1,0:T(2,128)(2,1)S(1)} %get-tuple-element.121), channel_id=15, replica_groups=mesh['fsdp'=32] {'fsdp'}, dimensions={1}, use_global_device_ids=true | all-gather | bytes 8448 | tf_op jit(solution)/shard_map/all_gather | solution.py:82
  539.7 4.8 fusion.644
  546.3 4.9 fusion.643
  558.4 8.2 broadcast_select_fusion.3
  568.9 3.0 fusion.108
  578.7 2.7 fusion.158
  583.2 4.7 fusion.71
  587.9 3.2 fusion.107
  598.4 11.2 %fusion.655 = (f32[32]{0:T(128)}, f32[32,1024]{1,0:T(8,128)}) fusion(f32[1024]{0:T(1024)} %convert_element_type.416, bf16[1,4096,1024]{2,1,0:T(8,128)(2,1)} %all-gather.34.cloned.1.call-done, bf16[1,1024,4096]{2,1,0:T(8,128)(2,1)} %all-gather.32.cloned.1.call-done, f32[4096]{0:T(1024)} %bitcast.399, f32[32,1024]{1,0:T(8,128)} %copy-done.20, ...), kind=kOutput, calls=%fused_computation.780 | convolution fusion | flops 545914880 | bytes 17068416 | tf_op jit(solution)/shard_map/dot_general | solution.py:26
  612.5 4.8 fusion.660
  624.5 4.7 fusion.46
  629.2 3.4 fusion.104
  639.9 2.7 fusion.157
  644.4 4.7 fusion.69
  649.0 3.0 fusion.103
  655.3 2.3 fusion.646
  658.2 10.6 %fusion.647 = (f32[32]{0:T(128)S(1)}, f32[32,1024]{1,0:T(8,128)}) fusion(f32[1024]{0:T(1024)} %convert_element_type.416, bf16[1,4096,1024]{2,1,0:T(8,128)(2,1)} %all-gather.34.cloned.1.call-done, bf16[1,1024,4096]{2,1,0:T(8,128)(2,1)} %all-gather.32.cloned.1.call-done, f32[4096]{0:T(1024)} %bitcast.400, f32[32,1024]{1,0:T(8,128)} %copy-done.18, ...), kind=kOutput, calls=%fused_computation.776 | convolution fusion | flops 545914880 | bytes 17068416 | tf_op jit(solution)/shard_map/dot_general | solution.py:26
  670.0 4.9 fusion.652
  679.8 8.4 broadcast_select_fusion.1
  688.2 2.3 fusion.42
  690.5 3.0 fusion.102
  696.7 2.3 fusion.668
  704.6 4.7 fusion.50
  709.2 3.0 fusion.106
  715.5 2.3 fusion.661
  719.0 2.7 fusion.160
  723.4 4.7 fusion.61
  728.1 3.0 fusion.101
  733.4 3.2 fusion.105
  741.1 2.3 fusion.669
  744.3 10.6 %fusion.670 = (f32[32]{0:T(128)S(1)}, f32[32,1024]{1,0:T(8,128)}) fusion(f32[1024]{0:T(1024)} %convert_element_type.417, bf16[1,4096,1024]{2,1,0:T(8,128)(2,1)} %all-gather.40.cloned.1.call-done, bf16[1,1024,4096]{2,1,0:T(8,128)(2,1)} %all-gather.38.cloned.1.call-done, f32[4096]{0:T(1024)} %bitcast.397, f32[32,1024]{1,0:T(8,128)} %copy-done.21, ...), kind=kOutput, calls=%fused_computation.787 | convolution fusion | flops 545914880 | bytes 17068416 | tf_op jit(solution)/shard_map/dot_general | solution.py:26
  756.6 3.5 fusion.59
  762.0 2.3 fusion.662
  765.2 10.6 %fusion.663 = (f32[32]{0:T(128)S(1)}, f32[32,1024]{1,0:T(8,128)}) fusion(f32[1024]{0:T(1024)} %convert_element_type.417, bf16[1,4096,1024]{2,1,0:T(8,128)(2,1)} %all-gather.40.cloned.1.call-done, bf16[1,1024,4096]{2,1,0:T(8,128)(2,1)} %all-gather.38.cloned.1.call-done, f32[4096]{0:T(1024)} %bitcast.398, f32[32,1024]{1,0:T(8,128)} %copy-done.19, ...), kind=kOutput, calls=%fused_computation.784 | convolution fusion | flops 545914880 | bytes 17068416 | tf_op jit(solution)/shard_map/dot_general | solution.py:26
  779.4 9.2 select_select_fusion.1
  788.7 6.9 pad_maximum_fusion.1
  795.6 36.5 %all-gather.28.cloned.1.call-done = bf16[1024,1024]{1,0:T(8,128)(2,1)} async-done(((bf16[32,1024]{1,0:T(8,128)(2,1)}), bf16[1024,1024]{1,0:T(8,128)(2,1)}) %all-gather.28.cloned.1.call-update) | async-done | bytes 2097168 | tf_op jit(solution)/shard_map/all_gather | solution.py:90
  832.1 7.1 add_bitcast_fusion
  839.1 50.9 %all-gather.26.cloned.1.call-done = bf16[1024,1024]{1,0:T(8,128)(2,1)} async-done(((bf16[32,1024]{1,0:T(8,128)(2,1)}), bf16[1024,1024]{1,0:T(8,128)(2,1)}) %all-gather.26.cloned.1.call-update) | async-done | bytes 2097168 | tf_op jit(solution)/shard_map/all_gather | solution.py:90
  890.1 7.0 add_bitcast_fusion.1
  897.1 12.1 %pad_maximum_fusion = f32[2,1024,1572]{1,2,0:T(8,128)} fusion(f32[1,1024,1572]{1,2,0:T(8,128)} %add_bitcast_fusion, f32[1,1024,1572]{1,2,0:T(8,128)} %add_bitcast_fusion.1), kind=kLoop, calls=%fused_computation.11 | loop fusion | flops 3219456 | bytes 25755648 | tf_op jit(solution)/shard_map/stack | solution.py:93
  909.2 34.0 %copy.78 = f32[2,1024,1572]{1,0,2:T(2,128)} copy(f32[2,1024,1572]{1,2,0:T(8,128)} %pad_maximum_fusion) | data formatting | bytes 25755648
  (313 shorter events, 110.9 us)
Async XLA Ops:
  7.2 46.1 %copy-start = (bf16[1572,1024]{1,0:T(8,128)(2,1)S(1)}, bf16[1572,1024]{1,0:T(8,128)(2,1)}, u32[]{:S(2)}) copy-start(bf16[1572,1024]{1,0:T(8,128)(2,1)} %param.36) | copy-start | bytes 9658372
  7.2 529.7 %reduce-scatter.2.cloned.1.call-start = ((), (), s32[]{:S(2)}) async-start(), calls=%async_computation.1 | async-start | bytes 4325376 | tf_op jit(solution)/shard_map/reduce_scatter | solution.py:70
  76.1 8.1 copy-start.49
  76.1 13.9 %copy-start.37 = (bf16[2,1024]{1,0:T(2,128)(2,1)S(1)}, bf16[2,1024]{1,0:T(2,128)(2,1)}, u32[]{:S(2)}) copy-start(bf16[2,1024]{1,0:T(2,128)(2,1)} %param.38) | copy-start | bytes 12292
  76.1 13.9 %copy-start.38 = (bf16[2,6,32]{2,0,1:T(2,128)(2,1)S(1)}, bf16[2,6,32]{2,0,1:T(2,128)(2,1)}, u32[]{:S(2)}) copy-start(bf16[2,6,32]{2,0,1:T(2,128)(2,1)} %param.29) | copy-start | bytes 2308
  76.2 463.5 %all-gather.30.cloned.1.call-start = ((), (), s32[]{:S(2)}) async-start(), calls=%async_computation.4 | async-start | bytes 12976128 | tf_op jit(solution)/shard_map/all_gather | solution.py:79
  78.3 66.4 %copy-start.39 = (bf16[2,3,32]{2,0,1:T(2,128)(2,1)S(1)}, bf16[2,3,32]{2,0,1:T(2,128)(2,1)}, u32[]{:S(2)}) copy-start(bf16[2,3,32]{2,0,1:T(2,128)(2,1)} %param.34) | copy-start | bytes 1156
  78.3 520.1 %all-gather.32.cloned.1.call-start = ((), (), s32[]{:S(2)}) async-start(), calls=%async_computation.5 | async-start | bytes 8650752 | tf_op jit(solution)/shard_map/all_gather | solution.py:81
  80.3 115.2 %copy-start.40 = (bf16[2,3,32]{2,0,1:T(2,128)(2,1)S(1)}, bf16[2,3,32]{2,0,1:T(2,128)(2,1)}, u32[]{:S(2)}) copy-start(bf16[2,3,32]{2,0,1:T(2,128)(2,1)} %param.35) | copy-start | bytes 1156
  80.3 518.2 %all-gather.34.cloned.1.call-start = ((), (), s32[]{:S(2)}) async-start(), calls=%async_computation.6 | async-start | bytes 8650752 | tf_op jit(solution)/shard_map/all_gather | solution.py:83
  82.2 530.3 %all-gather.36.cloned.1.call-start = ((), (), s32[]{:S(2)}) async-start(), calls=%async_computation.7 | async-start | bytes 12976128 | tf_op jit(solution)/shard_map/all_gather | solution.py:79
  82.8 661.5 %all-gather.38.cloned.1.call-start = ((), (), s32[]{:S(2)}) async-start(), calls=%async_computation.8 | async-start | bytes 8650752 | tf_op jit(solution)/shard_map/all_gather | solution.py:81
  83.4 660.9 %all-gather.40.cloned.1.call-start = ((), (), s32[]{:S(2)}) async-start(), calls=%async_computation.9 | async-start | bytes 8650752 | tf_op jit(solution)/shard_map/all_gather | solution.py:83
  84.1 747.9 %all-gather.28.cloned.1.call-start = ((), (), s32[]{:S(2)}) async-start(), calls=%async_computation.3 | async-start | bytes 2162688 | tf_op jit(solution)/shard_map/all_gather | solution.py:90
  84.2 453.8 %copy-start.41 = (pred[32]{0:T(512)(128)(4,1)}, pred[32]{0:T(512)(128)(4,1)S(1)}, u32[]{:S(2)}) copy-start(pred[32]{0:T(512)(128)(4,1)S(1)} %get-tuple-element.118) | copy-start | bytes 100
  84.2 455.4 %copy-start.42 = (pred[32]{0:T(512)(128)(4,1)}, pred[32]{0:T(512)(128)(4,1)S(1)}, u32[]{:S(2)}) copy-start(pred[32]{0:T(512)(128)(4,1)S(1)} %get-tuple-element.54) | copy-start | bytes 100
  87.5 452.2 %copy-start.9 = (bf16[32,1024]{1,0:T(8,128)(2,1)}, bf16[32,1024]{1,0:T(8,128)(2,1)S(1)}, u32[]{:S(2)}) copy-start(bf16[32,1024]{1,0:T(8,128)(2,1)S(1)} %gather_fusion.1) | copy-start | bytes 196612
  90.1 449.6 %copy-start.43 = (f32[1,1024]{1,0:T(1,128)}, f32[1,1024]{1,0:T(1,128)S(1)}, u32[]{:S(2)}) copy-start(f32[1,1024]{1,0:T(1,128)S(1)} %get-tuple-element.104) | copy-start | bytes 12292
  90.1 449.6 %copy-start.44 = (f32[1,1024]{1,0:T(1,128)}, f32[1,1024]{1,0:T(1,128)S(1)}, u32[]{:S(2)}) copy-start(f32[1,1024]{1,0:T(1,128)S(1)} %get-tuple-element.105) | copy-start | bytes 12292
  128.8 0.8 copy-start.1
  143.9 395.7 %copy-start.36 = (f32[1,3,1024]{2,1,0:T(4,128)}, f32[1,3,1024]{2,1,0:T(4,128)S(1)}, u32[]{:S(2)}) copy-start(f32[1,3,1024]{2,1,0:T(4,128)S(1)} %copy.192) | copy-start | bytes 36868
  235.8 18.5 %slice-start = ((s8[8388608]{0:T(1024)(128)(4,1)}), s8[4194304]{0:T(1024)(128)(4,1)S(1)}, s32[]{:S(2)}) async-start(s8[8388608]{0:T(1024)(128)(4,1)} %bitcast.375), calls=%async_computation.10 | async-start | bytes 8388608
  246.9 6.7 copy-start.61
  246.9 7.4 slice-start.1
  254.3 4.3 copy-start.50
  254.3 44.2 %copy-start.51 = (bf16[2,128]{1,0:T(2,128)(2,1)S(1)}, bf16[2,128]{1,0:T(2,128)(2,1)}, u32[]{:S(2)}) copy-start(bf16[2,128]{1,0:T(2,128)(2,1)} %param.31) | copy-start | bytes 1540
  379.8 0.8 copy-start.2
  537.9 7.2 copy-start.55
  538.0 7.2 copy-start.52
  539.1 6.0 copy-start.65
  558.4 8.2 copy-start.11
  566.6 2.3 copy-start.30
  583.2 4.7 copy-start.22
  583.2 8.1 copy-start.5
  597.1 0.8 copy-start.60
  624.5 4.7 copy-start.32
  624.5 8.3 copy-start.7
  638.7 10.4 %copy-start.23 = (pred[32,32]{1,0:T(8,128)(4,1)S(1)}, pred[32,32]{1,0:T(8,128)(4,1)}, u32[]{:S(2)}) copy-start(pred[32,32]{1,0:T(8,128)(4,1)} %iota_compare_fusion.2) | copy-start | bytes 3076
  644.3 7.9 copy-start.6
  658.2 11.8 %copy-start.13 = (f32[1,3,1024]{2,1,0:T(4,128)S(1)}, f32[1,3,1024]{2,1,0:T(4,128)}, u32[]{:S(2)}) copy-start(f32[1,3,1024]{2,1,0:T(4,128)} %copy.191) | copy-start | bytes 36868
  658.2 11.8 %copy-start.28 = (f32[1024]{0:T(1024)S(1)}, f32[1024]{0:T(1024)}, u32[]{:S(2)}) copy-start(f32[1024]{0:T(1024)} %get-tuple-element.31) | copy-start | bytes 12292
  658.2 11.8 %copy-start.29 = (f32[1024]{0:T(1024)S(1)}, f32[1024]{0:T(1024)}, u32[]{:S(2)}) copy-start(f32[1024]{0:T(1024)} %get-tuple-element.34) | copy-start | bytes 12292
  668.9 6.7 copy-start.48
  670.0 5.5 copy-start.57
  679.8 8.4 copy-start.12
  688.2 2.3 copy-start.33
  704.6 4.7 copy-start.31
  704.6 7.9 copy-start.8
  717.8 0.7 copy-start.14
  717.8 10.3 %copy-start.24 = (pred[32,32]{1,0:T(8,128)(4,1)S(1)}, pred[32,32]{1,0:T(8,128)(4,1)}, u32[]{:S(2)}) copy-start(pred[32,32]{1,0:T(8,128)(4,1)} %iota_compare_fusion.2) | copy-start | bytes 3076
  723.4 7.7 copy-start.4
  723.4 7.7 copy-start.10
  728.1 10.0 %copy-start.3 = (bf16[32,32,16,64]{3,2,1,0:T(8,128)(2,1)S(1)}, bf16[32,32,16,64]{3,2,1,0:T(8,128)(2,1)}, u32[]{:S(2)}) copy-start(bf16[32,32,16,64]{3,2,1,0:T(8,128)(2,1)} %get-tuple-element.65) | copy-start | bytes 6291460
  754.9 5.2 copy-start.27
  754.9 1.7 copy-start.46
  764.2 0.7 copy-start.19
  765.1 11.8 %copy-start.34 = (f32[1024]{0:T(1024)S(1)}, f32[1024]{0:T(1024)}, u32[]{:S(2)}) copy-start(f32[1024]{0:T(1024)} %get-tuple-element.22) | copy-start | bytes 12292
  765.1 11.8 %copy-start.35 = (f32[1024]{0:T(1024)S(1)}, f32[1024]{0:T(1024)}, u32[]{:S(2)}) copy-start(f32[1024]{0:T(1024)} %get-tuple-element.25) | copy-start | bytes 12292
  765.1 11.8 %copy-start.47 = (f32[32]{0:T(128)S(1)}, f32[32]{0:T(128)}, u32[]{:S(2)}) copy-start(f32[32]{0:T(128)} %copy-done.46) | copy-start | bytes 388
  765.1 11.8 %copy-start.56 = (f32[32]{0:T(128)S(1)}, f32[32]{0:T(128)}, u32[]{:S(2)}) copy-start(f32[32]{0:T(128)} %add_rsqrt_fusion) | copy-start | bytes 388
  765.1 14.3 %copy-start.25 = (pred[32,32]{1,0:T(8,128)(4,1)S(1)}, pred[32,32]{1,0:T(8,128)(4,1)}, u32[]{:S(2)}) copy-start(pred[32,32]{1,0:T(8,128)(4,1)} %iota_compare_fusion.3) | copy-start | bytes 3076
  765.1 14.3 %copy-start.26 = (pred[32,32]{1,0:T(8,128)(4,1)S(1)}, pred[32,32]{1,0:T(8,128)(4,1)}, u32[]{:S(2)}) copy-start(pred[32,32]{1,0:T(8,128)(4,1)} %get-tuple-element.113) | copy-start | bytes 3076
  778.7 111.4 %all-gather.26.cloned.1.call-start = ((), (), s32[]{:S(2)}) async-start(), calls=%async_computation.2 | async-start | bytes 2162688 | tf_op jit(solution)/shard_map/all_gather | solution.py:90
  788.7 43.4 %copy-start.62 = (f32[1572]{0:T(1024)S(1)}, f32[1572]{0:T(1024)}, u32[]{:S(2)}) copy-start(f32[1572]{0:T(1024)} %param.39) | copy-start | bytes 18868
  (15 other events, 9.3 us)
Sparse Core Ops, SparseCore 0:
  76.3 139.1 reduce-scatter.1
  218.3 91.9 all-gather.29
  313.2 77.3 all-gather.31
  393.3 80.5 all-gather.33
  476.7 95.2 all-gather.35
  574.7 75.1 all-gather.37
  652.8 76.0 all-gather.39
  778.8 53.2 all-gather.27
  834.9 55.0 all-gather.25
where the time goes:
time: 956 us; the launch traced here: 950 us
  blocking collectives  398 us (42%)
  other arithmetic  178 us (19%)
  matrix products  147 us (15%)
  local copies, waits for them, and re-layouts  122 us (13%)
  waiting for transfers between devices  90 us (9%)
  between operations  15.3 us (2%)
    all_gather x2, waiting for transfers between devices, local_decode(): lax.all_gather(hidden.astype(jnp.bfloat16), 'fsdp', axis=0, tiled=True)  87.4 us
    all_gather x2, blocking collectives, local_decode(): ln_shifts = lax.all_gather(ln_bias[layer_idx], 'fsdp', axis=1, tiled=True)  80.5 us
    all_gather x2, blocking collectives, local_decode(): layer_b = lax.all_gather(attn_b[layer_idx], 'fsdp', axis=1, tiled=True)  79.1 us
    all_gather x2, blocking collectives, local_decode(): ln_gains = lax.all_gather(ln_gain[layer_idx], 'fsdp', axis=1, tiled=True)  78.9 us
    all_gather x2, blocking collectives, local_decode(): up_b = lax.all_gather(fc1_b[layer_idx], 'fsdp', axis=0, tiled=True)  77.4 us
    dot_general x16, matrix products, project(): jnp.dot(act_rows, weight, preferred_element_type=jnp.float32)  71.3 us
    unnamed x156, local copies, waits for them, and re-layouts  46.3 us
    all_gather x1, blocking collectives, local_decode(): all_tokens = lax.all_gather(tokens, 'fsdp', axis=0, tiled=True)  43.5 us
  transfers between devices with their start and end apart: 9, of which 2 were waited for; matrix products, arithmetic and copies ran while one was open for 34% of the time, Pallas kernels for 0%

commit v1 on v0

v1 whole, which is shorter than its diff:
```python
import functools

import jax
import jax.numpy as jnp
from jax import lax
from jax.experimental import pallas as pl
from jax.experimental.pallas import tpu as pltpu
from jax.sharding import PartitionSpec as P

LN_EPS = 1e-5


MESH = pl.DeviceIdType.MESH
ORDER_E, ORDER_A, ORDER_B = 'xyz', 'zxy', 'zyx'
NUM_Z = 4
OFFSETS = [(dz, fx, fy) for dz in range(1 - NUM_Z, NUM_Z) for fx in (0, 1) for fy in (0, 1)]


class Grid:
    def __init__(self):
        self.me = lax.axis_index('fsdp')
        self.z = self.me // 8
        self.step_x = 2 - 4 * ((self.me // 2) % 2)
        self.step_y = 4 - 8 * ((self.me // 4) % 2)
        self.step_core = 1 - 2 * (self.me % 2)

    def source(self, offset):
        dz, fx, fy = offset
        return self.me + 8 * dz + fx * self.step_x + fy * self.step_y

    def exists(self, dz):
        if dz > 0:
            return self.z < NUM_Z - dz
        return self.z >= -dz

    def barrier(self):
        sem = pltpu.get_barrier_semaphore()
        for step in (self.step_x, self.step_y, self.step_core):
            pl.semaphore_signal(sem, inc=1, device_id=(self.me + step,), device_id_type=MESH)
        for dz in (1, -1):
            @pl.when(self.exists(dz))
            def _():
                pl.semaphore_signal(sem, inc=1, device_id=(self.me + 8 * dz,), device_id_type=MESH)
        inner = jnp.logical_and(self.z > 0, self.z < NUM_Z - 1)

        @pl.when(inner)
        def _():
            pl.semaphore_wait(sem, 5)

        @pl.when(jnp.logical_not(inner))
        def _():
            pl.semaphore_wait(sem, 4)


def onward(offset, order):
    dz, fx, fy = offset
    parts = {'x': fx, 'y': fy, 'z': dz}
    last = max([place for place, dim in enumerate(order) if parts[dim]], default=-1)
    sends = [('c', 0)]
    if last >= 0 and order[last] == 'z':
        sends.append(('u', 1) if dz < 0 else ('d', -1))
    for dim in order[last + 1:]:
        sends += [('u', 1), ('d', -1)] if dim == 'z' else [(dim, 0)]
    return sends


def hops(offset):
    return abs(offset[0]) + offset[1] + offset[2]


WAYS = 'xyudc'


class Gather:
    def __init__(self, grid, pieces, send_sem, recv_sem):
        self.grid, self.pieces, self.send_sem, self.recv_sem = grid, pieces, send_sem, recv_sem

    def copy(self, number, offset, way):
        grid = self.grid
        source = grid.source(offset)
        own, place, _ = self.pieces[number]
        step = {'x': grid.step_x, 'y': grid.step_y, 'u': 8, 'd': -8, 'c': grid.step_core}[way]
        here = place(source)
        return pltpu.make_async_remote_copy(
            src_ref=own if hops(offset) == 0 else here, dst_ref=here,
            send_sem=self.send_sem.at[number, source // 2, WAYS.index(way)], recv_sem=self.recv_sem.at[number, source],
            device_id=(grid.me + step,), device_id_type=MESH)

    def each_send(self, number, offset, act):
        for way, dz in onward(offset, self.pieces[number][2]):
            if dz:
                @pl.when(self.grid.exists(dz))
                def _(way=way):
                    act(self.copy(number, offset, way))
            else:
                act(self.copy(number, offset, way))

    def forward(self, number, count):
        for offset in OFFSETS:
            if hops(offset) != count:
                continue

            def pass_on(offset=offset):
                if count:
                    self.wait(number, self.grid.source(offset))
                self.each_send(number, offset, lambda copy: copy.start())

            if offset[0]:
                pl.when(self.grid.exists(offset[0]))(pass_on)
            else:
                pass_on()

    def wait(self, number, source):
        place = self.pieces[number][1](source)
        pltpu.make_async_remote_copy(
            src_ref=place, dst_ref=place, send_sem=self.recv_sem.at[number, source], recv_sem=self.recv_sem.at[number, source],
            device_id=(self.grid.me,), device_id_type=MESH).wait_recv()

    def finish(self, number):
        other = self.grid.step_core
        for offset in OFFSETS:
            def drain(offset=offset):
                self.wait(number, self.grid.source(offset) + other)
                self.each_send(number, offset, lambda copy: copy.wait_send())

            if offset[0]:
                pl.when(self.grid.exists(offset[0]))(drain)
            else:
                drain()


MAX_HOPS = NUM_Z + 1
WEIGHT_GROUPS = ((0, 3, ORDER_E), (3, 5, ORDER_A), (8, 6, ORDER_B))


def weights_kernel(in_ref, out_ref, send_sem, recv_sem, own_sem):
    grid = Grid()
    num_layers, num_blocks, share, _ = in_ref.shape

    def piece(layer, first, count, order):
        return (in_ref.at[layer, pl.ds(first, count)],
                lambda source: out_ref.at[layer, pl.ds(first, count), pl.ds(pl.multiple_of(share * source, share), share), :], order)

    pieces = [piece(layer, *group) for layer in range(num_layers) for group in WEIGHT_GROUPS]
    gather = Gather(grid, pieces, send_sem, recv_sem)
    own = pltpu.make_async_copy(in_ref, out_ref.at[:, :, pl.ds(pl.multiple_of(share * grid.me, share), share), :], own_sem)
    own.start()
    grid.barrier()
    per_layer = len(WEIGHT_GROUPS)
    for count in range(MAX_HOPS + 2):
        for number in range(len(pieces)):
            hop = count - number // per_layer
            if 0 <= hop <= MAX_HOPS:
                gather.forward(number, hop)
    for number in range(len(pieces)):
        gather.finish(number)
    own.wait()


def gather_weights(packed):
    num_layers, num_blocks, share, width = packed.shape
    num_pieces = num_layers * len(WEIGHT_GROUPS)
    return pl.pallas_call(
        weights_kernel,
        out_shape=jax.ShapeDtypeStruct((num_layers, num_blocks, share * 32, width), packed.dtype),
        in_specs=[pl.BlockSpec(memory_space=pl.ANY)],
        out_specs=pl.BlockSpec(memory_space=pl.ANY),
        scratch_shapes=[pltpu.SemaphoreType.DMA((num_pieces, 16, len(WAYS))), pltpu.SemaphoreType.DMA((num_pieces, 32)), pltpu.SemaphoreType.DMA],
        compiler_params=pltpu.CompilerParams(collective_id=1, has_side_effects=True),
        cost_estimate=pl.CostEstimate(flops=200_000_000_000, bytes_accessed=120_000_000, transcendentals=0),
        name='gather_weights',
    )(packed)


def layer_norm(values, gain_row, shift_row):
    row_mean = values.mean(-1, keepdims=True)
    centered = values - row_mean
    variance = (centered * centered).mean(-1, keepdims=True)
    return centered * lax.rsqrt(variance + LN_EPS) * gain_row.astype(jnp.float32) + shift_row.astype(jnp.float32)


def attend(query_rows, key_rows, val_rows, valid_len):
    scores = jnp.einsum('sbhd,bthd->sbht', query_rows, key_rows, preferred_element_type=jnp.float32)
    valid_mask = jnp.arange(key_rows.shape[1])[None, None, None, :] < valid_len[:, :, None, None]
    scores = jnp.where(valid_mask, scores, -jnp.inf)
    weights = jnp.exp(scores - scores.max(-1, keepdims=True))
    mixed_rows = jnp.einsum('sbht,bthd->sbhd', weights.astype(jnp.bfloat16), val_rows, preferred_element_type=jnp.float32)
    return mixed_rows / weights.sum(-1)[:, :, :, None]


def project(act_rows, weight, bias_row):
    return jnp.einsum('...d,de->...e', act_rows, weight, preferred_element_type=jnp.float32) + bias_row


def decoder_layer(hidden, positions, src_len, cache_k, cache_v, cross_k, cross_v, layer_w, layer_b, up_w, up_b, down_w, down_b, ln_gains, ln_shifts):
    num_rows, num_times, num_heads, head_dim = cache_k.shape
    num_steps = hidden.shape[0]
    attn_scale = head_dim ** -0.5
    head_shape = (num_steps, num_rows, num_heads, head_dim)
    act_rows = hidden.astype(jnp.bfloat16)
    self_query = (project(act_rows, layer_w[0], layer_b[0]) * attn_scale).astype(jnp.bfloat16).reshape(head_shape)
    new_key = project(act_rows, layer_w[1], layer_b[1]).astype(jnp.bfloat16).reshape(head_shape)
    new_val = project(act_rows, layer_w[2], layer_b[2]).astype(jnp.bfloat16).reshape(head_shape)
    times = jnp.arange(num_times)[None, :]
    for step in range(num_steps):
        write_mask = (times == positions[:, None] + step)[:, :, None, None]
        cache_k = jnp.where(write_mask, new_key[step][:, None], cache_k)
        cache_v = jnp.where(write_mask, new_val[step][:, None], cache_v)
    steps = jnp.arange(num_steps)[:, None]
    mixed_rows = attend(self_query, cache_k, cache_v, positions[None, :] + steps + 1)
    attn_out = project(mixed_rows.reshape(hidden.shape).astype(jnp.bfloat16), layer_w[3], layer_b[3])
    hidden = layer_norm(hidden + attn_out, ln_gains[0], ln_shifts[0])
    cross_query = (project(hidden.astype(jnp.bfloat16), layer_w[4], layer_b[4]) * attn_scale).astype(jnp.bfloat16).reshape(head_shape)
    mixed_rows = attend(cross_query, cross_k, cross_v, jnp.broadcast_to(src_len[None], (num_steps, num_rows)))
    cross_out = project(mixed_rows.reshape(hidden.shape).astype(jnp.bfloat16), layer_w[5], layer_b[5])
    hidden = layer_norm(hidden + cross_out, ln_gains[1], ln_shifts[1])
    inner = jnp.einsum('sbd,ide->sbie', hidden.astype(jnp.bfloat16), up_w, preferred_element_type=jnp.float32) + up_b.reshape(4, -1)
    inner_act = jax.nn.gelu(inner, approximate=False).astype(jnp.bfloat16)
    ffn_out = jnp.einsum('sbie,ied->sbd', inner_act, down_w, preferred_element_type=jnp.float32) + down_b
    hidden = layer_norm(hidden + ffn_out, ln_gains[2], ln_shifts[2])
    return hidden, cache_k, cache_v


def solution(mesh):
    cache_spec = P(None, 'fsdp')
    in_specs = (P('fsdp'), P('fsdp'), P('fsdp'), cache_spec, cache_spec, cache_spec, cache_spec,
                P(None, None, 'fsdp'), P(None, None, 'fsdp'), P(None, 'fsdp'), P(None, 'fsdp'),
                P(None, 'fsdp'), P(None, 'fsdp'), P(None, None, 'fsdp'), P(None, None, 'fsdp'),
                P('fsdp'), P(), P(), P('fsdp'))
    out_specs = (P(None, None, 'fsdp'), cache_spec, cache_spec)

    def local_decode(tokens, positions, src_len, self_k, self_v, cross_k, cross_v, attn_w, attn_b, fc1_w, fc1_b, fc2_w, fc2_b, ln_gain, ln_bias, tok_embed, pos_embed, emb_norm, logit_bias):
        shard_idx = lax.axis_index('fsdp')
        num_layers = attn_w.shape[0]
        num_rows, num_steps = tokens.shape
        vocab_local = tok_embed.shape[0]
        small = (tokens.T, attn_b, fc1_b, fc2_b, ln_gain, ln_bias)
        packed = jnp.concatenate([part.astype(jnp.float32).reshape(-1) for part in small])
        gathered = lax.all_gather(packed, 'fsdp', axis=0)
        pieces, start = [], 0
        for part in small:
            block = gathered[:, start:start + part.size].reshape((-1,) + part.shape)
            pieces.append(jnp.moveaxis(block, 0, -2).reshape(part.shape[:-1] + (-1,)))
            start += part.size
        all_tokens = pieces[0].astype(jnp.int32)
        all_attn_b, all_fc1_b, all_fc2_b, all_gain, all_shift = pieces[1:]
        local_ids = all_tokens - shard_idx * vocab_local
        owned_mask = (local_ids >= 0) & (local_ids < vocab_local)
        picked = jnp.take(tok_embed, jnp.clip(local_ids, 0, vocab_local - 1), axis=0)
        picked = jnp.where(owned_mask[:, :, None], picked, jnp.zeros_like(picked))
        tok_rows = lax.psum_scatter(picked, 'fsdp', scatter_dimension=1, tiled=True)
        step_pos = positions[None, :] + jnp.arange(num_steps)[:, None]
        start_rows = tok_rows.astype(jnp.float32) + jnp.take(pos_embed, step_pos + 2, axis=0).astype(jnp.float32)
        hidden = layer_norm(start_rows, emb_norm[0], emb_norm[1])
        num_dev = mesh.shape['fsdp']
        depth = attn_w.shape[2]
        width = attn_w.shape[3]
        up_blocks = fc1_w.reshape(num_layers, depth, num_dev, 4, depth).transpose(0, 3, 1, 2, 4).reshape(num_layers, 4, depth, width)
        down_blocks = fc2_w.reshape(num_layers, 4, depth, width)
        packed_w = jnp.concatenate([attn_w[:, :3], attn_w[:, 4:5], up_blocks, attn_w[:, 3:4], attn_w[:, 5:6], down_blocks], axis=1)
        full_w = gather_weights(packed_w)
        all_fc1_b = all_fc1_b.reshape(num_layers, num_dev, 4, depth).transpose(0, 2, 1, 3).reshape(num_layers, 4 * width)
        cache_k, cache_v = [], []
        for layer_idx in range(num_layers):
            blocks = full_w[layer_idx]
            layer_w = (blocks[0], blocks[1], blocks[2], blocks[8], blocks[3], blocks[9])
            up_w, down_w = blocks[4:8], blocks[10:14]
            hidden, new_k, new_v = decoder_layer(
                hidden, positions, src_len, self_k[layer_idx], self_v[layer_idx], cross_k[layer_idx], cross_v[layer_idx],
                layer_w, all_attn_b[layer_idx], up_w, all_fc1_b[layer_idx], down_w, all_fc2_b[layer_idx], all_gain[layer_idx], all_shift[layer_idx])
            cache_k.append(new_k)
            cache_v.append(new_v)
        all_rows = lax.all_gather(hidden.astype(jnp.bfloat16), 'fsdp', axis=1, tiled=True)
        logits = jnp.einsum('vd,sbd->vsb', tok_embed, all_rows, preferred_element_type=jnp.float32) + logit_bias[:, None, None]
        return jnp.transpose(logits, (1, 2, 0)), jnp.stack(cache_k), jnp.stack(cache_v)

    return jax.shard_map(local_decode, mesh=mesh, in_specs=in_specs, out_specs=out_specs, check_vma=False)
```

time: 956 us -> 646 us (0.68)
  blocking collectives: 398 us -> 43.7 us
  Pallas kernels: 0 us -> 245 us
  other arithmetic: 178 us -> 81.8 us
  waiting for transfers between devices: 90 us -> 26.7 us
  matrix products: 147 us -> 84 us
  local copies, waits for them, and re-layouts: 122 us -> 141 us
    all_gather x9 -> x1, blocking collectives: 360 us -> 43.7 us  [local_decode(): gathered = lax.all_gather(packed, 'fsdp', axis=0)]
    pallas_call x0 -> x1, Pallas kernels: none -> 245 us  [gather_weights(): pl.pallas_call(weights_kernel, out_shape=jax.ShapeDtypeStruct((num_layers...]
    dot_general x38 -> x25, matrix products: 147 us -> 84 us  [the longest x12 26.7 us: project(): jnp.einsum('...d,de->...e', act_rows, weight, preferred_element_type=jnp....]
    all_gather x8 -> x1, waiting for transfers between devices: 87.4 us -> 26.7 us  [local_decode(): lax.all_gather(hidden.astype(jnp.bfloat16), 'fsdp', axis=1, tiled=True)]
    add x5 -> x2, other arithmetic: 48.1 us -> 0.66 us  [the longest x1 0.66 us: decoder_layer(): write_mask = (times == positions[:, None] + step)[:, :, None, None]]
    unnamed x1 -> x0, blocking collectives: 38.8 us -> none
    sub x8 -> x0, other arithmetic: 25.1 us -> none  [attend(): weights = jnp.exp(scores - scores.max(-1, keepdims=True))]
    add x0 -> x23, local copies, waits for them, and re-layouts: none -> 23.6 us  [the longest x12 11.9 us: project(): jnp.einsum('...d,de->...e', act_rows, weight, preferred_element_type=jnp....]
  transfers between devices with their start and end apart: 9 -> 2, of which waited for: 2 -> 1; matrix products, arithmetic and copies ran while one was open for 34% -> 18% of each run, Pallas kernels for 0% -> 38%
where the time goes in v1:
time: 646 us; the launch traced here: 637 us
  Pallas kernels  245 us (38%)
  local copies, waits for them, and re-layouts  141 us (22%)
  matrix products  84 us (13%)
  other arithmetic  81.8 us (13%)
  blocking collectives  43.7 us (7%)
  waiting for transfers between devices  26.7 us (4%)
  between operations  15.4 us (2%)
    pallas_call x1, Pallas kernels, gather_weights(): pl.pallas_call(weights_kernel, out_shape=jax.ShapeDtypeStruct((num_layers...  245 us
    all_gather x1, blocking collectives, local_decode(): gathered = lax.all_gather(packed, 'fsdp', axis=0)  43.7 us
    unnamed x119, local copies, waits for them, and re-layouts  29.8 us
    dot_general x12, matrix products, project(): jnp.einsum('...d,de->...e', act_rows, weight, preferred_element_type=jnp....  26.7 us
    all_gather x1, waiting for transfers between devices, local_decode(): lax.all_gather(hidden.astype(jnp.bfloat16), 'fsdp', axis=1, tiled=True)  26.7 us
    select_n x1, other arithmetic, decoder_layer(): cache_v = jnp.where(write_mask, new_val[step][:, None], cache_v)  14.8 us
    dot_general x4, matrix products, attend(): jnp.einsum('sbhd,bthd->sbht', query_rows, key_rows, preferred_element_typ...  14.3 us
    select_n x2, other arithmetic, decoder_layer(): cache_k = jnp.where(write_mask, new_key[step][:, None], cache_k)  14.3 us
  transfers between devices with their start and end apart: 2, of which 1 were waited for; matrix products, arithmetic and copies ran while one was open for 18% of the time, Pallas kernels for 38%

profile of v1, /device:TPU:0, one launch (start us, length us, event | category | flops | bytes accessed | tf_op | source)
XLA Modules:
  0.0 637.3 jit_solution(6721438181491085619)
XLA Ops:
  12.0 43.7 %all-gather.1 = f32[32,1,1152]{2,1,0:T(1,128)S(1)} all-gather(f32[1,1,1152]{2,1,0:T(1,128)S(1)} %reshape.598), channel_id=2, replica_groups=mesh['fsdp'=32] {'fsdp'}, dimensions={0}, use_global_device_ids=true | all-gather | bytes 152064 | tf_op jit(solution)/shard_map/all_gather | solution.py:239
  58.8 9.6 %gather_fusion = bf16[2048,1024]{1,0:T(8,128)(2,1)} fusion(bf16[1572,1024]{1,0:T(8,128)(2,1)S(1)} %copy-done, s32[2048]{0:T(1024)S(1)} %bitcast_clamp_fusion), kind=kCustom, calls=%fused_computation | custom fusion | bytes 8396800 | tf_op jit(solution)/shard_map/jit(_take)/gather | solution.py:249
  68.4 3.9 select_select_fusion.4
  72.4 1.8 slice_dynamic-update-slice_fusion
  74.2 1.6 slice_dynamic-update-slice_fusion.3
  75.8 3.5 reshape.547
  79.2 3.3 copy.275
  82.5 4.2 reshape.548
  86.7 1.9 constant_dynamic-update-slice_fusion.1
  90.2 1.6 slice_dynamic-update-slice_fusion.1
  91.7 1.9 constant_dynamic-update-slice_fusion.in_ref
  93.6 244.6 %gather_weights.1 = bf16[2,14,1024,1024]{3,2,1,0:T(8,128)(2,1)} custom-call(bf16[2,14,32,1024]{3,2,1,0:T(8,128)(2,1)} %constant_dynamic-update-slice_fusion.in_ref), custom_call_target="tpu_custom_call" | custom-call | flops 199999995904 | bytes 120000000 | tf_op jit(solution)/shard_map/gather_weights/pallas_call | solution.py:163
  339.9 1.6 slice.411
  345.9 1.6 fusion.401
  378.0 2.7 gather_fusion.1
  386.9 7.2 %fusion.399 = (bf16[1,32,32,16,64]{4,3,2,1,0:T(8,128)(2,1)}, bf16[1,32,32,16,64]{4,3,2,1,0:T(8,128)(2,1)}) fusion(bf16[2,32,32,16,64]{4,3,2,1,0:T(8,128)(2,1)} %param.24), kind=kLoop, calls=%fused_computation.441 | loop fusion | bytes 8388608 | tf_op jit(solution)/shard_map/slice | solution.py:269
  394.0 6.7 %fusion.400 = (bf16[1,32,32,16,64]{4,3,2,1,0:T(8,128)(2,1)}, bf16[1,32,32,16,64]{4,3,2,1,0:T(8,128)(2,1)}) fusion(bf16[2,32,32,16,64]{4,3,2,1,0:T(8,128)(2,1)} %param.25), kind=kLoop, calls=%fused_computation.442 | loop fusion | bytes 8388608 | tf_op jit(solution)/shard_map/slice | solution.py:269
  404.6 2.7 fusion.172
  407.4 2.1 fusion.175
  409.4 2.1 fusion.178
  413.8 1.6 broadcast_in_dim.224
  415.5 1.7 broadcast_in_dim.232
  417.9 1.8 reshape.551
  419.7 7.1 %fusion.18 = (bf16[32,32,16,64]{3,2,1,0:T(8,128)(2,1)S(1)}, bf16[32,32,16,64]{3,2,1,0:T(8,128)(2,1)S(1)}) fusion(pred[32,32]{1,0:T(8,128)(4,1)} %get-tuple-element.107, pred[32,32]{1,0:T(8,128)(4,1)} %get-tuple-element.108, bf16[2,32,32,16,64]{4,3,2,1,0:T(8,128)(2,1)} %param.22, bf16[32,16,64]{2,1,0:T(8,128)(2,1)} %broadcast_in_dim.232, ...), kind=kLoop, calls=%fused_computation.30 | loop fusion | flops 4194304 | bytes 8652800 | tf_op jit(solution)/shard_map/jit(_where)/select_n | solution.py:207
  426.9 2.4 fusion.408
  429.2 2.1 fusion.275
  431.3 2.2 fusion.24
  434.7 2.0 fusion.214
  436.7 1.8 convert_element_type.160
  438.5 2.2 fusion.409
  441.4 2.1 fusion.169
  444.4 4.8 fusion.410
  449.2 2.1 fusion.277
  451.3 2.4 fusion.14
  454.9 2.0 fusion.213
  458.0 2.2 fusion.411
  460.5 5.3 fusion.297
  465.8 6.0 fusion.412
  472.2 2.7 fusion.160
  474.9 2.1 fusion.163
  477.0 2.1 fusion.166
  481.4 1.7 broadcast_in_dim.236
  483.1 1.6 broadcast_in_dim.242
  485.6 1.8 reshape.557
  487.4 7.1 %fusion.16 = (bf16[32,32,16,64]{3,2,1,0:T(8,128)(2,1)S(1)}, bf16[32,32,16,64]{3,2,1,0:T(8,128)(2,1)S(1)}) fusion(pred[32,32]{1,0:T(8,128)(4,1)} %get-tuple-element.107, pred[32,32]{1,0:T(8,128)(4,1)} %get-tuple-element.108, bf16[2,32,32,16,64]{4,3,2,1,0:T(8,128)(2,1)} %param.22, bf16[32,16,64]{2,1,0:T(8,128)(2,1)} %broadcast_in_dim.242, ...), kind=kLoop, calls=%fused_computation.26 | loop fusion | flops 4194304 | bytes 8652800 | tf_op jit(solution)/shard_map/jit(_where)/select_n | solution.py:207
  494.6 2.4 fusion.413
  496.9 2.1 fusion.279
  499.0 2.4 fusion.20
  502.6 2.0 fusion.212
  505.8 2.2 fusion.414
  508.7 2.1 fusion.157
  511.7 4.8 fusion.415
  516.5 2.1 fusion.281
  518.6 2.2 fusion.12
  522.0 2.0 fusion.211
  525.1 2.2 fusion.416
  527.6 5.3 fusion.298
  532.9 6.0 fusion.417
  540.0 14.8 %select_select_fusion.1 = (bf16[1,32,32,16,64]{4,3,2,1,0:T(8,128)(2,1)}, bf16[1,32,32,16,64]{4,3,2,1,0:T(8,128)(2,1)}, bf16[1,32,32,16,64]{4,3,2,1,0:T(8,128)(2,1)}, bf16[1,32,32,16,64]{4,3,2,1,0:T(8,128)(2,1)}) fusion(pred[32,32]{1,0:T(8,128)(4,1)S(1)} %copy-done.10, pred[32,32]{1,0:T(8,128)(4,1)S(1)} %copy-done.11, bf16[2,32,32,16,64]{4,3,2,1,0:T(8,128)(2,1)} %param.23, ...), kind=kLoop, calls=%fused_computation.42 | loop fusion | flops 8388608 | bytes 17303552 | tf_op jit(solution)/shard_map/jit(_where)/select_n | solution.py:208
  554.8 8.8 %pad_maximum_fusion.1 = bf16[2,32,32,16,64]{4,3,2,1,0:T(8,128)(2,1)} fusion(bf16[1,32,32,16,64]{4,3,2,1,0:T(8,128)(2,1)} %get-tuple-element.50, bf16[1,32,32,16,64]{4,3,2,1,0:T(8,128)(2,1)} %get-tuple-element.49), kind=kLoop, calls=%fused_computation.3 | loop fusion | flops 2097152 | bytes 8388608 | tf_op jit(solution)/shard_map/stack | solution.py:275
  563.5 8.8 %pad_maximum_fusion = bf16[2,32,32,16,64]{4,3,2,1,0:T(8,128)(2,1)} fusion(bf16[1,32,32,16,64]{4,3,2,1,0:T(8,128)(2,1)} %get-tuple-element.71, bf16[1,32,32,16,64]{4,3,2,1,0:T(8,128)(2,1)} %get-tuple-element.72), kind=kLoop, calls=%fused_computation.2 | loop fusion | flops 2097152 | bytes 8388608 | tf_op jit(solution)/shard_map/stack | solution.py:275
  572.3 26.7 %all-gather.4.cloned.1.call-done = bf16[2,1024,1024]{2,1,0:T(8,128)(2,1)} async-done(((bf16[2,32,1024]{2,1,0:T(8,128)(2,1)}), bf16[2,1024,1024]{2,1,0:T(8,128)(2,1)}) %all-gather.4.cloned.1.call-update) | async-done | bytes 4194320 | tf_op jit(solution)/shard_map/all_gather | solution.py:273
  599.0 11.3 %broadcast_add_fusion = f32[2,1024,1572]{1,2,0:T(8,128)S(1)} fusion(f32[1572]{0:T(1024)S(1)} %copy-done.55, bf16[2,1024,1024]{2,1,0:T(8,128)(2,1)} %all-gather.4.cloned.1.call-done, bf16[1572,1024]{1,0:T(8,128)(2,1)S(1)} %copy-done), kind=kOutput, calls=%fused_computation.16 | convolution fusion | flops 6596665344 | bytes 20297872 | tf_op jit(solution)/shard_map/vd,sbd->vsb/dot_general | solution.py:274
  610.3 19.7 %copy.199 = f32[2,1024,1572]{1,0,2:T(2,128)} copy(f32[2,1024,1572]{1,2,0:T(8,128)S(1)} %broadcast_add_fusion) | data formatting | bytes 25755648
  (237 shorter events, 75.5 us)
Async XLA Ops:
  7.2 51.6 %copy-start = (bf16[1572,1024]{1,0:T(8,128)(2,1)S(1)}, bf16[1572,1024]{1,0:T(8,128)(2,1)}, u32[]{:S(2)}) copy-start(bf16[1572,1024]{1,0:T(8,128)(2,1)} %param.34) | copy-start | bytes 9658372
  7.2 393.6 %reduce-scatter.2.cloned.1.call-start = ((), (), s32[]{:S(2)}) async-start(), calls=%async_computation.1 | async-start | bytes 4325376 | tf_op jit(solution)/shard_map/reduce_scatter | solution.py:251
  72.4 526.6 %all-gather.4.cloned.1.call-start = ((), (), s32[]{:S(2)}) async-start(), calls=%async_computation.2 | async-start | bytes 4325376 | tf_op jit(solution)/shard_map/all_gather | solution.py:273
  93.6 247.9 %copy-start.54 = (s32[32]{0:T(128)S(1)}, s32[32]{0:T(128)}, u32[]{:S(2)}) copy-start(s32[32]{0:T(128)} %param.20) | copy-start | bytes 388
  381.3 21.7 %copy-start.32 = (pred[2,32]{1,0:T(4,128)(4,1)}, pred[2,32]{1,0:T(4,128)(4,1)S(1)}, u32[]{:S(2)}) copy-start(pred[2,32]{1,0:T(4,128)(4,1)S(1)} %compare_and_fusion.2) | copy-start | bytes 196
  384.1 18.9 %copy-start.18 = (f32[1,1024]{1,0:T(1,128)}, f32[1,1024]{1,0:T(1,128)S(1)}, u32[]{:S(2)}) copy-start(f32[1,1024]{1,0:T(1,128)S(1)} %get-tuple-element.77) | copy-start | bytes 12292
  384.1 18.9 %copy-start.20 = (f32[1,1024]{1,0:T(1,128)}, f32[1,1024]{1,0:T(1,128)S(1)}, u32[]{:S(2)}) copy-start(f32[1,1024]{1,0:T(1,128)S(1)} %get-tuple-element.78) | copy-start | bytes 12292
  401.8 1.2 copy-start.28
  403.0 0.6 copy-start.34
  419.7 7.1 %copy-start.6 = (bf16[2,32,16,64]{3,2,1,0:T(8,128)(2,1)S(1)}, bf16[2,32,16,64]{3,2,1,0:T(8,128)(2,1)}, u32[]{:S(2)}) copy-start(bf16[2,32,16,64]{3,2,1,0:T(8,128)(2,1)} %reshape.551) | copy-start | bytes 393220
  419.7 7.1 %copy-start.26 = (pred[2,32,32]{2,0,1:T(4,128)(4,1)S(1)}, pred[2,32,32]{2,0,1:T(4,128)(4,1)}, u32[]{:S(2)}) copy-start(pred[2,32,32]{2,0,1:T(4,128)(4,1)} %iota_compare_fusion.1) | copy-start | bytes 6148
  431.3 7.2 %copy-start.19 = (f32[1,1024]{1,0:T(1,128)S(1)}, f32[1,1024]{1,0:T(1,128)}, u32[]{:S(2)}) copy-start(f32[1,1024]{1,0:T(1,128)} %copy-done.18) | copy-start | bytes 12292
  431.3 7.2 %copy-start.21 = (f32[1,1024]{1,0:T(1,128)S(1)}, f32[1,1024]{1,0:T(1,128)}, u32[]{:S(2)}) copy-start(f32[1,1024]{1,0:T(1,128)} %copy-done.20) | copy-start | bytes 12292
  431.3 7.2 %copy-start.29 = (f32[2,32]{1,0:T(2,128)S(1)}, f32[2,32]{1,0:T(2,128)}, u32[]{:S(2)}) copy-start(f32[2,32]{1,0:T(2,128)} %copy-done.28) | copy-start | bytes 772
  431.3 7.2 %copy-start.33 = (pred[2,32]{1,0:T(4,128)(4,1)S(1)}, pred[2,32]{1,0:T(4,128)(4,1)}, u32[]{:S(2)}) copy-start(pred[2,32]{1,0:T(4,128)(4,1)} %copy-done.32) | copy-start | bytes 196
  433.5 10.9 %copy-start.24 = (pred[2,32,32]{2,0,1:T(4,128)(4,1)S(1)}, pred[2,32,32]{2,0,1:T(4,128)(4,1)}, u32[]{:S(2)}) copy-start(pred[2,32,32]{2,0,1:T(4,128)(4,1)} %iota_compare_fusion) | copy-start | bytes 6148
  440.7 0.7 copy-start.9
  444.4 6.9 %copy-start.2 = (bf16[1,32,32,16,64]{4,3,2,1,0:T(8,128)(2,1)S(1)}, bf16[1,32,32,16,64]{4,3,2,1,0:T(8,128)(2,1)}, u32[]{:S(2)}) copy-start(bf16[1,32,32,16,64]{4,3,2,1,0:T(8,128)(2,1)} %get-tuple-element.55) | copy-start | bytes 6291460
  451.3 6.7 %copy-start.51 = (f32[1024]{0:T(1024)S(1)}, f32[1024]{0:T(1024)}, u32[]{:S(2)}) copy-start(f32[1024]{0:T(1024)} %add.470) | copy-start | bytes 12292
  451.3 6.7 %copy-start.52 = (f32[1024]{0:T(1024)S(1)}, f32[1024]{0:T(1024)}, u32[]{:S(2)}) copy-start(f32[1024]{0:T(1024)} %mul.188) | copy-start | bytes 12292
  451.3 6.7 %copy-start.53 = (f32[1024]{0:T(1024)S(1)}, f32[1024]{0:T(1024)}, u32[]{:S(2)}) copy-start(f32[1024]{0:T(1024)} %add.476) | copy-start | bytes 12292
  451.3 9.1 %copy-start.23 = (f32[4,1024]{1,0:T(4,128)S(1)}, f32[4,1024]{1,0:T(4,128)}, u32[]{:S(2)}) copy-start(f32[4,1024]{1,0:T(4,128)} %add.484) | copy-start | bytes 49156
  451.3 9.1 %copy-start.46 = (f32[1024]{0:T(1024)S(1)}, f32[1024]{0:T(1024)}, u32[]{:S(2)}) copy-start(f32[1024]{0:T(1024)} %add.481) | copy-start | bytes 12292
  451.3 9.1 %copy-start.47 = (f32[1024]{0:T(1024)S(1)}, f32[1024]{0:T(1024)}, u32[]{:S(2)}) copy-start(f32[1024]{0:T(1024)} %mul.195) | copy-start | bytes 12292
  460.5 5.3 copy-start.43
  465.8 6.3 copy-start.14
  465.8 6.3 copy-start.16
  465.8 6.4 %copy-start.48 = (f32[1024]{0:T(1024)S(1)}, f32[1024]{0:T(1024)}, u32[]{:S(2)}) copy-start(f32[1024]{0:T(1024)} %add.501) | copy-start | bytes 12292
  465.8 9.1 %copy-start.49 = (f32[1024]{0:T(1024)S(1)}, f32[1024]{0:T(1024)}, u32[]{:S(2)}) copy-start(f32[1024]{0:T(1024)} %add.498) | copy-start | bytes 12292
  471.8 7.3 %copy-start.5 = (f32[2,32,1024]{2,1,0:T(8,128)}, f32[2,32,1024]{2,1,0:T(8,128)S(1)}, u32[]{:S(2)}) copy-start(f32[2,32,1024]{2,1,0:T(8,128)S(1)} %get-tuple-element.89) | copy-start | bytes 786436
  471.8 5.2 copy-start.50
  471.9 7.3 %copy-start.30 = (f32[2,32]{1,0:T(2,128)}, f32[2,32]{1,0:T(2,128)S(1)}, u32[]{:S(2)}) copy-start(f32[2,32]{1,0:T(2,128)S(1)} %broadcast_multiply_fusion.3) | copy-start | bytes 772
  472.1 7.7 %copy-start.35 = (f32[2,32]{1,0:T(2,128)}, f32[2,32]{1,0:T(2,128)S(1)}, u32[]{:S(2)}) copy-start(f32[2,32]{1,0:T(2,128)S(1)} %add_rsqrt_fusion.3) | copy-start | bytes 772
  481.4 13.1 %copy-start.4 = (bf16[32,16,64]{2,1,0:T(8,128)(2,1)}, bf16[32,16,64]{2,1,0:T(8,128)(2,1)S(1)}, u32[]{:S(2)}) copy-start(bf16[32,16,64]{2,1,0:T(8,128)(2,1)S(1)} %broadcast_in_dim.240) | copy-start | bytes 196612
  487.4 7.2 %copy-start.7 = (bf16[2,32,16,64]{3,2,1,0:T(8,128)(2,1)S(1)}, bf16[2,32,16,64]{3,2,1,0:T(8,128)(2,1)}, u32[]{:S(2)}) copy-start(bf16[2,32,16,64]{3,2,1,0:T(8,128)(2,1)} %reshape.557) | copy-start | bytes 393220
  487.4 7.2 %copy-start.27 = (pred[2,32,32]{2,0,1:T(4,128)(4,1)S(1)}, pred[2,32,32]{2,0,1:T(4,128)(4,1)}, u32[]{:S(2)}) copy-start(pred[2,32,32]{2,0,1:T(4,128)(4,1)} %iota_compare_fusion.1) | copy-start | bytes 6148
  499.0 6.8 %copy-start.15 = (f32[1024]{0:T(1024)S(1)}, f32[1024]{0:T(1024)}, u32[]{:S(2)}) copy-start(f32[1024]{0:T(1024)} %add.492) | copy-start | bytes 12292
  499.0 6.8 %copy-start.17 = (f32[1024]{0:T(1024)S(1)}, f32[1024]{0:T(1024)}, u32[]{:S(2)}) copy-start(f32[1024]{0:T(1024)} %mul.204) | copy-start | bytes 12292
  499.0 6.8 %copy-start.31 = (f32[2,32]{1,0:T(2,128)S(1)}, f32[2,32]{1,0:T(2,128)}, u32[]{:S(2)}) copy-start(f32[2,32]{1,0:T(2,128)} %copy-done.30) | copy-start | bytes 772
  499.0 6.8 %copy-start.36 = (f32[2,32]{1,0:T(2,128)S(1)}, f32[2,32]{1,0:T(2,128)}, u32[]{:S(2)}) copy-start(f32[2,32]{1,0:T(2,128)} %copy-done.35) | copy-start | bytes 772
  499.0 6.8 %copy-start.45 = (f32[1024]{0:T(1024)S(1)}, f32[1024]{0:T(1024)}, u32[]{:S(2)}) copy-start(f32[1024]{0:T(1024)} %add.504) | copy-start | bytes 12292
  501.4 7.3 %copy-start.40 = (f32[1024]{0:T(1024)S(1)}, f32[1024]{0:T(1024)}, u32[]{:S(2)}) copy-start(f32[1024]{0:T(1024)} %add.509) | copy-start | bytes 12292
  501.4 7.3 %copy-start.41 = (f32[1024]{0:T(1024)S(1)}, f32[1024]{0:T(1024)}, u32[]{:S(2)}) copy-start(f32[1024]{0:T(1024)} %mul.211) | copy-start | bytes 12292
  501.4 7.3 %copy-start.44 = (f32[1024]{0:T(1024)S(1)}, f32[1024]{0:T(1024)}, u32[]{:S(2)}) copy-start(f32[1024]{0:T(1024)} %add.512) | copy-start | bytes 12292
  501.4 10.3 %copy-start.25 = (pred[2,32,32]{2,0,1:T(4,128)(4,1)S(1)}, pred[2,32,32]{2,0,1:T(4,128)(4,1)}, u32[]{:S(2)}) copy-start(pred[2,32,32]{2,0,1:T(4,128)(4,1)} %iota_compare_fusion) | copy-start | bytes 6148
  508.0 0.7 copy-start.8
  511.7 6.9 %copy-start.1 = (bf16[1,32,32,16,64]{4,3,2,1,0:T(8,128)(2,1)S(1)}, bf16[1,32,32,16,64]{4,3,2,1,0:T(8,128)(2,1)}, u32[]{:S(2)}) copy-start(bf16[1,32,32,16,64]{4,3,2,1,0:T(8,128)(2,1)} %get-tuple-element.56) | copy-start | bytes 6291460
  518.6 6.5 %copy-start.42 = (f32[1024]{0:T(1024)S(1)}, f32[1024]{0:T(1024)}, u32[]{:S(2)}) copy-start(f32[1024]{0:T(1024)} %add.515) | copy-start | bytes 12292
  518.6 8.9 %copy-start.22 = (f32[4,1024]{1,0:T(4,128)S(1)}, f32[4,1024]{1,0:T(4,128)}, u32[]{:S(2)}) copy-start(f32[4,1024]{1,0:T(4,128)} %add.523) | copy-start | bytes 49156
  518.6 8.9 %copy-start.38 = (f32[1024]{0:T(1024)S(1)}, f32[1024]{0:T(1024)}, u32[]{:S(2)}) copy-start(f32[1024]{0:T(1024)} %add.520) | copy-start | bytes 12292
  518.6 8.9 %copy-start.39 = (f32[1024]{0:T(1024)S(1)}, f32[1024]{0:T(1024)}, u32[]{:S(2)}) copy-start(f32[1024]{0:T(1024)} %mul.218) | copy-start | bytes 12292
  527.5 5.3 copy-start.37
  532.9 6.3 copy-start.12
  532.9 6.3 copy-start.13
  532.9 7.1 %copy-start.3 = (bf16[32,16,64]{2,1,0:T(8,128)(2,1)S(1)}, bf16[32,16,64]{2,1,0:T(8,128)(2,1)}, u32[]{:S(2)}) copy-start(bf16[32,16,64]{2,1,0:T(8,128)(2,1)} %broadcast_in_dim.224) | copy-start | bytes 196612
  532.9 7.1 %copy-start.10 = (pred[32,32]{1,0:T(8,128)(4,1)S(1)}, pred[32,32]{1,0:T(8,128)(4,1)}, u32[]{:S(2)}) copy-start(pred[32,32]{1,0:T(8,128)(4,1)} %get-tuple-element.107) | copy-start | bytes 3076
  532.9 7.1 %copy-start.11 = (pred[32,32]{1,0:T(8,128)(4,1)S(1)}, pred[32,32]{1,0:T(8,128)(4,1)}, u32[]{:S(2)}) copy-start(pred[32,32]{1,0:T(8,128)(4,1)} %get-tuple-element.108) | copy-start | bytes 3076
  563.5 35.4 %copy-start.55 = (f32[1572]{0:T(1024)S(1)}, f32[1572]{0:T(1024)}, u32[]{:S(2)}) copy-start(f32[1572]{0:T(1024)} %param.37) | copy-start | bytes 18868
Sparse Core Ops, SparseCore 0:
  72.5 143.4 reduce-scatter.1
  540.1 58.8 all-gather.3

commit v2 on v0

v2 whole, which is shorter than its diff:
```python
import functools

import jax
import jax.numpy as jnp
from jax import lax
from jax.experimental import pallas as pl
from jax.experimental.pallas import tpu as pltpu
from jax.sharding import PartitionSpec as P

LN_EPS = 1e-5


MESH = pl.DeviceIdType.MESH
ORDER_E, ORDER_A, ORDER_B = 'xyz', 'zxy', 'zyx'
NUM_Z = 4
OFFSETS = [(dz, fx, fy) for dz in range(1 - NUM_Z, NUM_Z) for fx in (0, 1) for fy in (0, 1)]


class Grid:
    def __init__(self):
        self.me = lax.axis_index('fsdp')
        self.z = self.me // 8
        self.step_x = 2 - 4 * ((self.me // 2) % 2)
        self.step_y = 4 - 8 * ((self.me // 4) % 2)
        self.step_core = 1 - 2 * (self.me % 2)

    def source(self, offset):
        dz, fx, fy = offset
        return self.me + 8 * dz + fx * self.step_x + fy * self.step_y

    def exists(self, dz):
        if dz > 0:
            return self.z < NUM_Z - dz
        return self.z >= -dz

    def neighbour_barrier(self):
        sem = pltpu.get_barrier_semaphore()
        for step in (self.step_x, self.step_y, self.step_core):
            pl.semaphore_signal(sem, inc=1, device_id=(self.me + step,), device_id_type=MESH)
        for dz in (1, -1):
            @pl.when(self.exists(dz))
            def _():
                pl.semaphore_signal(sem, inc=1, device_id=(self.me + 8 * dz,), device_id_type=MESH)
        inner = jnp.logical_and(self.z > 0, self.z < NUM_Z - 1)

        @pl.when(inner)
        def _():
            pl.semaphore_wait(sem, 5)

        @pl.when(jnp.logical_not(inner))
        def _():
            pl.semaphore_wait(sem, 4)


NUM_DEV = 32


class Exchange:
    def __init__(self, block, place, send_sem, recv_sem):
        self.me = lax.axis_index('fsdp')
        self.block, self.place, self.send_sem, self.recv_sem = block, place, send_sem, recv_sem

    def peer(self, step):
        return lax.rem(self.me + step, NUM_DEV)

    def copy(self, step, source):
        peer = self.peer(step)
        return pltpu.make_async_remote_copy(
            src_ref=self.block(peer), dst_ref=self.place(source), send_sem=self.send_sem.at[step], recv_sem=self.recv_sem.at[source],
            device_id=(peer,), device_id_type=MESH)

    def signal(self):
        barrier = pltpu.get_barrier_semaphore()

        @pl.loop(1, NUM_DEV)
        def _(step):
            pl.semaphore_signal(barrier, inc=1, device_id=(self.peer(step),), device_id_type=MESH)

    def barrier(self):
        pl.semaphore_wait(pltpu.get_barrier_semaphore(), NUM_DEV - 1)

    def start(self):
        @pl.loop(1, NUM_DEV)
        def _(step):
            self.copy(step, self.me).start()

    def wait_recv(self):
        @pl.loop(1, NUM_DEV)
        def _(step):
            self.copy(step, self.peer(step)).wait_recv()

    def wait_send(self):
        @pl.loop(1, NUM_DEV)
        def _(step):
            self.copy(step, self.me).wait_send()


def onward(offset, order):
    dz, fx, fy = offset
    parts = {'x': fx, 'y': fy, 'z': dz}
    last = max([place for place, dim in enumerate(order) if parts[dim]], default=-1)
    sends = [('c', 0)]
    if last >= 0 and order[last] == 'z':
        sends.append(('u', 1) if dz < 0 else ('d', -1))
    for dim in order[last + 1:]:
        sends += [('u', 1), ('d', -1)] if dim == 'z' else [(dim, 0)]
    return sends


def hops(offset):
    return abs(offset[0]) + offset[1] + offset[2]


WAYS = 'xyudc'


MAX_HOPS = NUM_Z + 1


class Gather:
    def __init__(self, grid, pieces, waves, send_sem, recv_sem):
        self.grid, self.pieces, self.waves, self.send_sem, self.recv_sem = grid, pieces, waves, send_sem, recv_sem

    def copy(self, wave, number, piece, offset, way):
        grid = self.grid
        source = grid.source(offset)
        own, place, _ = piece
        step = {'x': grid.step_x, 'y': grid.step_y, 'u': 8, 'd': -8, 'c': grid.step_core}[way]
        here = place(source)
        return pltpu.make_async_remote_copy(
            src_ref=own if hops(offset) == 0 else here, dst_ref=here,
            send_sem=self.send_sem.at[wave, number, source // 2, WAYS.index(way)], recv_sem=self.recv_sem.at[wave, number, source],
            device_id=(grid.me + step,), device_id_type=MESH)

    def each_send(self, wave, number, piece, offset, act):
        for way, dz in onward(offset, piece[2]):
            if dz:
                @pl.when(self.grid.exists(dz))
                def _(way=way):
                    act(self.copy(wave, number, piece, offset, way))
            else:
                act(self.copy(wave, number, piece, offset, way))

    def wait(self, wave, number, piece, source):
        place = piece[1](source)
        pltpu.make_async_remote_copy(
            src_ref=place, dst_ref=place, send_sem=self.recv_sem.at[wave, number, source], recv_sem=self.recv_sem.at[wave, number, source],
            device_id=(self.grid.me,), device_id_type=MESH).wait_recv()

    def each_offset(self, count, act):
        for offset in OFFSETS:
            if count is None or hops(offset) == count:
                if offset[0]:
                    pl.when(self.grid.exists(offset[0]))(functools.partial(act, offset))
                else:
                    act(offset)

    def forward(self, wave, count):
        for number, piece in enumerate(self.pieces(wave)):
            def pass_on(offset, number=number, piece=piece):
                if count:
                    self.wait(wave, number, piece, self.grid.source(offset))
                self.each_send(wave, number, piece, offset, lambda copy: copy.start())

            self.each_offset(count, pass_on)

    def run(self, first=True):
        if first:
            self.forward(0, 0)

        def cross(wave, carry):
            for count in range(1, MAX_HOPS + 1):
                if count == 3 and self.waves > 1:
                    @pl.when(wave + 1 < self.waves)
                    def _():
                        self.forward(wave + 1, 0)
                self.forward(wave, count)
            return carry

        def finish(wave, carry):
            for number, piece in enumerate(self.pieces(wave)):
                def drain(offset, number=number, piece=piece):
                    self.wait(wave, number, piece, self.grid.source(offset) + self.grid.step_core)
                    self.each_send(wave, number, piece, offset, lambda copy: copy.wait_send())

                self.each_offset(None, drain)
            return carry

        lax.fori_loop(0, self.waves, cross, 0)
        lax.fori_loop(0, self.waves, finish, 0)


def rows_at(ref, lead, share):
    return lambda source: ref.at[(*lead, pl.ds(pl.multiple_of(share * source, share), share))]


ROW_FC2, ROW_GAIN, ROW_SHIFT, ROW_TOKEN, ROW_FC1 = 12, 14, 20, 26, 28
SLOTS = 16


def weights_kernel(small, tail, embed_hbm, attn_ref, fc1_ref, fc2_ref, table_out, rows_out, attn_out, fc1_out, fc2_out,
                   ids, ranks, onehot, picks, embed, send_sem, recv_sem, own_sem, small_send, small_recv, row_send, row_recv):
    grid = Grid()
    me = grid.me
    num_layers = attn_ref.shape[0]
    share = small.shape[1]
    table = Exchange(lambda peer: small, lambda source: table_out.at[source], small_send, small_recv)
    rows = Exchange(lambda peer: picks.at[peer], lambda source: rows_out.at[source], row_send, row_recv)
    table.signal()

    def pieces(layer):
        blocks = [(attn_ref.at[layer, pl.ds(first, count)], rows_at(attn_out, (layer, pl.ds(first, count)), attn_ref.shape[2]), order)
                  for first, count, order in ((0, 3, ORDER_E), (5, 1, ORDER_A), (3, 2, ORDER_B))]
        return blocks + [(fc1_ref.at[layer], rows_at(fc1_out, (layer,), fc1_ref.shape[1]), ORDER_A),
                         (fc2_ref.at[layer], rows_at(fc2_out, (layer,), fc2_ref.shape[1]), ORDER_B)]

    own = [
        pltpu.make_async_copy(attn_ref, rows_at(attn_out, (slice(None), slice(None)), attn_ref.shape[2])(me), own_sem.at[0]),
        pltpu.make_async_copy(fc1_ref, rows_at(fc1_out, (slice(None),), fc1_ref.shape[1])(me), own_sem.at[1]),
        pltpu.make_async_copy(fc2_ref, rows_at(fc2_out, (slice(None),), fc2_ref.shape[1])(me), own_sem.at[2]),
    ]
    for copy in own:
        copy.start()
    vocab = embed_hbm.shape[0]
    body = embed.shape[0] - tail.shape[0]
    embed_copy = pltpu.make_async_copy(embed_hbm.at[pl.ds(0, body)], embed.at[pl.ds(0, body)], own_sem.at[3])
    embed_copy.start()
    embed[pl.ds(body, tail.shape[0])] = tail[...]
    table_out[me] = small[...]
    table.barrier()
    table.start()
    gather = Gather(grid, pieces, num_layers, send_sem, recv_sem)
    gather.forward(0, 0)

    table.wait_recv()
    wanted = jnp.concatenate([table_out[:, ROW_TOKEN + step, :] for step in range(ids.shape[1] // share)], axis=1) - (me * vocab).astype(jnp.float32)
    mine = jnp.logical_and(wanted >= 0, wanted < vocab)
    number = ids.shape[1]
    before = lax.broadcasted_iota(jnp.int32, (number, number), 0) <= lax.broadcasted_iota(jnp.int32, (number, number), 1)
    rank = jnp.dot(jnp.where(mine, 1.0, 0.0).astype(jnp.bfloat16), jnp.where(before, 1.0, 0.0).astype(jnp.bfloat16), preferred_element_type=jnp.float32)
    ids[pl.ds(0, NUM_DEV)] = wanted
    ranks[pl.ds(0, NUM_DEV)] = jnp.where(mine, rank, 0.0)
    slot = lax.broadcasted_iota(jnp.int32, (SLOTS, number), 0).astype(jnp.float32) + 1.0
    line = lax.broadcasted_iota(jnp.int32, (SLOTS, embed.shape[0]), 1).astype(jnp.float32)

    @pl.loop(0, NUM_DEV)
    def _(peer):
        hit = ranks[pl.ds(peer, 1), :] == slot
        chosen = jnp.sum(jnp.where(hit, ids[pl.ds(peer, 1), :] + 1.0, 0.0), axis=1, keepdims=True)
        onehot[pl.ds(pl.multiple_of(peer * SLOTS, SLOTS), SLOTS), :] = jnp.where(line == chosen - 1.0, 1.0, 0.0).astype(jnp.bfloat16)

    group = 128 // SLOTS
    embed_copy.wait()

    @pl.loop(0, NUM_DEV // group)
    def _(part):
        found = jnp.dot(onehot[pl.ds(pl.multiple_of(part * 128, 128), 128), :], embed[...], preferred_element_type=jnp.float32)
        picks[pl.ds(part * group, group)] = found.astype(jnp.bfloat16).reshape(group, SLOTS, found.shape[1])

    rows_out[me] = picks[me]
    rows.start()
    gather.run(first=False)
    rows.wait_recv()
    rows.wait_send()
    table.wait_send()
    for copy in own:
        copy.wait()


def gather_weights(small, num_tokens, embed, attn_w, fc1_w, fc2_w):
    lanes = 128
    body = embed.shape[0] // lanes * lanes
    tail = jnp.zeros((lanes, embed.shape[1]), embed.dtype).at[:embed.shape[0] - body].set(embed[body:])
    def whole(array, dim):
        return jax.ShapeDtypeStruct(array.shape[:dim] + (array.shape[dim] * NUM_DEV,) + array.shape[dim + 1:], array.dtype)

    any_spec = pl.BlockSpec(memory_space=pl.ANY)
    vmem = pl.BlockSpec(memory_space=pltpu.VMEM)
    num_layers = attn_w.shape[0]
    width = embed.shape[1]
    dma = pltpu.SemaphoreType.DMA
    return pl.pallas_call(
        weights_kernel,
        out_shape=(jax.ShapeDtypeStruct((NUM_DEV,) + small.shape, jnp.float32), jax.ShapeDtypeStruct((NUM_DEV, SLOTS, width), embed.dtype),
                   whole(attn_w, 2), whole(fc1_w, 1), whole(fc2_w, 1)),
        in_specs=[vmem] * 2 + [any_spec] * 4,
        out_specs=(vmem, vmem) + (any_spec,) * 3,
        scratch_shapes=[
            pltpu.VMEM((NUM_DEV + 8, num_tokens), jnp.float32), pltpu.VMEM((NUM_DEV + 8, num_tokens), jnp.float32),
            pltpu.VMEM((NUM_DEV * SLOTS, body + lanes), jnp.bfloat16), pltpu.VMEM((NUM_DEV, SLOTS, width), jnp.bfloat16), pltpu.VMEM((body + lanes, width), jnp.bfloat16),
            dma((num_layers, 5, 16, len(WAYS))), dma((num_layers, 5, NUM_DEV)), dma((4,)),
            dma((NUM_DEV,)), dma((NUM_DEV,)), dma((NUM_DEV,)), dma((NUM_DEV,)),
        ],
        compiler_params=pltpu.CompilerParams(collective_id=1, has_side_effects=True, vmem_limit_bytes=40 * 1024 * 1024),
        cost_estimate=pl.CostEstimate(flops=200_000_000_000, bytes_accessed=120_000_000, transcendentals=0),
        name='gather_weights',
    )(small, tail, embed, attn_w, fc1_w, fc2_w)


def rows_kernel(in_ref, out_ref, send_sem, recv_sem, own_sem):
    grid = Grid()
    share = in_ref.shape[1]
    half = share // 2

    def piece(step, part, order):
        return (in_ref.at[step, pl.ds(part * half, half)],
                lambda source: out_ref.at[step, pl.ds(pl.multiple_of(share * source + part * half, half), half)], order)

    own = pltpu.make_async_copy(in_ref, out_ref.at[:, pl.ds(pl.multiple_of(share * grid.me, share), share)], own_sem)
    own.start()
    grid.neighbour_barrier()
    Gather(grid, lambda wave: [piece(0, 0, 'xzy'), piece(0, 1, 'yzx'), piece(1, 0, ORDER_A), piece(1, 1, ORDER_B)], 1, send_sem, recv_sem).run()
    own.wait()


def gather_rows(rows):
    steps, share, width = rows.shape
    vmem = pl.BlockSpec(memory_space=pltpu.VMEM)
    return pl.pallas_call(
        rows_kernel,
        out_shape=jax.ShapeDtypeStruct((steps, share * 32, width), rows.dtype),
        in_specs=[vmem],
        out_specs=vmem,
        scratch_shapes=[pltpu.SemaphoreType.DMA((1, 4, 16, len(WAYS))), pltpu.SemaphoreType.DMA((1, 4, 32)), pltpu.SemaphoreType.DMA],
        compiler_params=pltpu.CompilerParams(collective_id=2, has_side_effects=True),
        cost_estimate=pl.CostEstimate(flops=20_000_000_000, bytes_accessed=8_000_000, transcendentals=0),
        name='gather_rows',
    )(rows)


def norm_rows(values, gain_row, shift_row):
    row_mean = jnp.mean(values, axis=-1, keepdims=True)
    centered = values - row_mean
    variance = jnp.mean(centered * centered, axis=-1, keepdims=True)
    return centered * lax.rsqrt(variance + LN_EPS) * gain_row + shift_row


UNROLL = 4


def layers_kernel(pos_ref, len_ref, tok_ref, posrow_ref, embnorm_ref, table_ref, fc1b_ref, attn_hbm, fc1_hbm, fc2_hbm,
                  self_k_hbm, self_v_hbm, cross_k_hbm, cross_v_hbm, rows_ref, out_k_hbm, out_v_hbm,
                  attn_buf, fc1_buf, fc2_buf, kbuf, vbuf, ckbuf, cvbuf, q3, k3, v3, o3, xs, inner, w_sem, c_sem, o_sem):
    num_layers, num_rows, num_times, num_heads, head_dim = kbuf.shape
    num_steps = xs.shape[0] // num_rows
    width = xs.shape[1]
    fat = num_steps * num_heads

    def weight_copy(layer, which):
        if which < 6:
            return pltpu.make_async_copy(attn_hbm.at[layer, which], attn_buf.at[which], w_sem.at[which])
        if which == 6:
            return pltpu.make_async_copy(fc1_hbm.at[layer], fc1_buf, w_sem.at[6])
        return pltpu.make_async_copy(fc2_hbm.at[layer], fc2_buf, w_sem.at[7])

    def self_copy(layer):
        return (pltpu.make_async_copy(self_k_hbm.at[layer], kbuf.at[layer], c_sem.at[0, layer]),
                pltpu.make_async_copy(self_v_hbm.at[layer], vbuf.at[layer], c_sem.at[1, layer]))

    def cross_copy(layer):
        return (pltpu.make_async_copy(cross_k_hbm.at[layer], ckbuf, c_sem.at[2, 0]),
                pltpu.make_async_copy(cross_v_hbm.at[layer], cvbuf, c_sem.at[2, 1]))

    def out_copy(layer):
        return (pltpu.make_async_copy(kbuf.at[layer], out_k_hbm.at[layer], o_sem.at[0, layer]),
                pltpu.make_async_copy(vbuf.at[layer], out_v_hbm.at[layer], o_sem.at[1, layer]))

    for which in (0, 1, 2):
        weight_copy(0, which).start()
    for copy in self_copy(0):
        copy.start()
    for which in (3, 4):
        weight_copy(0, which).start()
    for copy in cross_copy(0):
        copy.start()
    for which in (5, 6, 7):
        weight_copy(0, which).start()
    for layer in range(1, num_layers):
        for copy in self_copy(layer):
            copy.start()

    gain = embnorm_ref[pl.ds(0, 1), :].astype(jnp.float32)
    shift = embnorm_ref[pl.ds(1, 1), :].astype(jnp.float32)
    xs[...] = norm_rows(tok_ref[...].astype(jnp.float32) + posrow_ref[...].astype(jnp.float32), gain, shift)

    row_id = lax.broadcasted_iota(jnp.int32, (fat, num_times * num_heads), 0)
    col_id = lax.broadcasted_iota(jnp.int32, (fat, num_times * num_heads), 1)
    same_head = lax.rem(row_id, num_heads) == lax.rem(col_id, num_heads)
    step_id, time_id = row_id // num_heads, col_id // num_heads
    self_rank = jnp.where(same_head, time_id - step_id, num_times * 2)
    cross_rank = jnp.where(same_head, time_id, num_times * 2)

    def row(index):
        return table_ref[pl.ds(index, 1), :]

    def project(values, which, layer):
        out = jnp.dot(values, attn_buf[which], preferred_element_type=jnp.float32) + row(layer * 6 + which)
        return out

    def refill(layer, which):
        @pl.when(layer + 1 < num_layers)
        def _():
            weight_copy(layer + 1, which).start()

    def split_heads(values, ref):
        for head in range(num_heads):
            ref[:, head, :] = values[:, head * head_dim:(head + 1) * head_dim]

    def join_heads(ref):
        return jnp.concatenate([ref[:, head, :] for head in range(num_heads)], axis=1)

    def per_step(ref, index):
        return jnp.concatenate([ref[step * num_rows + index] for step in range(num_steps)], axis=0)

    def attend_one(index, keys, vals, rank, last):
        query = per_step(q3, index).astype(jnp.bfloat16)
        keys = keys.reshape(num_times * num_heads, head_dim)
        vals = vals.reshape(num_times * num_heads, head_dim)
        scores = lax.dot_general(query, keys, (((1,), (1,)), ((), ())), preferred_element_type=jnp.float32)
        scores = jnp.where(rank <= last, scores, -jnp.inf)
        weights = jnp.exp(scores - jnp.max(scores, axis=-1, keepdims=True))
        total = jnp.sum(weights, axis=-1, keepdims=True)
        mixed = jnp.dot(weights.astype(jnp.bfloat16), vals, preferred_element_type=jnp.float32) / total
        for step in range(num_steps):
            o3[step * num_rows + index] = mixed[step * num_heads:(step + 1) * num_heads]

    def layer_body(layer, carry):
        scale = head_dim ** -0.5
        act = xs[...].astype(jnp.bfloat16)
        for which, ref in ((0, q3), (1, k3), (2, v3)):
            weight_copy(layer, which).wait()
            out = project(act, which, layer)
            split_heads(out * scale if which == 0 else out, ref)
            refill(layer, which)
        for copy in self_copy(layer):
            copy.wait()

        def self_group(group, carry):
            for lane in range(UNROLL):
                index = group * UNROLL + lane
                pos = pos_ref[index]
                for step in range(num_steps):
                    kbuf[layer, index, pos + step] = k3[step * num_rows + index].astype(jnp.bfloat16)
                    vbuf[layer, index, pos + step] = v3[step * num_rows + index].astype(jnp.bfloat16)
                attend_one(index, kbuf[layer, index], vbuf[layer, index], self_rank, pos)
            return carry

        lax.fori_loop(0, num_rows // UNROLL, self_group, 0)
        for copy in out_copy(layer):
            copy.start()
        weight_copy(layer, 3).wait()
        mixed = join_heads(o3).astype(jnp.bfloat16)
        out = project(mixed, 3, layer)
        refill(layer, 3)
        xs[...] = norm_rows(xs[...] + out, row(ROW_GAIN + layer * 3), row(ROW_SHIFT + layer * 3))

        weight_copy(layer, 4).wait()
        split_heads(project(xs[...].astype(jnp.bfloat16), 4, layer) * scale, q3)
        refill(layer, 4)
        for copy in cross_copy(layer):
            copy.wait()

        def cross_group(group, carry):
            for lane in range(UNROLL):
                index = group * UNROLL + lane
                attend_one(index, ckbuf[index], cvbuf[index], cross_rank, len_ref[index] - 1)
            return carry

        lax.fori_loop(0, num_rows // UNROLL, cross_group, 0)

        @pl.when(layer + 1 < num_layers)
        def _():
            for copy in cross_copy(layer + 1):
                copy.start()

        weight_copy(layer, 5).wait()
        mixed = join_heads(o3).astype(jnp.bfloat16)
        out = project(mixed, 5, layer)
        refill(layer, 5)
        xs[...] = norm_rows(xs[...] + out, row(ROW_GAIN + layer * 3 + 1), row(ROW_SHIFT + layer * 3 + 1))

        weight_copy(layer, 6).wait()
        act = xs[...].astype(jnp.bfloat16)
        tile = 512

        def up_tile(index, carry):
            cols = pl.ds(pl.multiple_of(index * tile, tile), tile)
            out = jnp.dot(act, fc1_buf[:, cols], preferred_element_type=jnp.float32) + fc1b_ref[pl.ds(layer, 1), cols]
            inner[:, cols] = (0.5 * out * (1.0 + lax.erf(out * (2.0 ** -0.5)))).astype(jnp.bfloat16)
            return carry

        lax.fori_loop(0, fc1_buf.shape[1] // tile, up_tile, 0)
        refill(layer, 6)
        weight_copy(layer, 7).wait()

        def down_tile(index, total):
            cols = pl.ds(pl.multiple_of(index * tile, tile), tile)
            return total + jnp.dot(inner[:, cols], fc2_buf[cols, :], preferred_element_type=jnp.float32)

        out = lax.fori_loop(0, fc2_buf.shape[0] // tile, down_tile, jnp.zeros(xs.shape, jnp.float32)) + row(ROW_FC2 + layer)
        refill(layer, 7)
        xs[...] = norm_rows(xs[...] + out, row(ROW_GAIN + layer * 3 + 2), row(ROW_SHIFT + layer * 3 + 2))
        return carry

    lax.fori_loop(0, num_layers, layer_body, 0)
    rows_ref[...] = xs[...].astype(jnp.bfloat16)
    for layer in range(num_layers):
        for copy in out_copy(layer):
            copy.wait()


def run_layers(positions, src_len, tok_rows, pos_rows, emb_norm, table, fc1_b, attn_full, fc1_full, fc2_full, self_k, self_v, cross_k, cross_v):
    smem = pl.BlockSpec(memory_space=pltpu.SMEM)
    vmem = pl.BlockSpec(memory_space=pltpu.VMEM)
    any_spec = pl.BlockSpec(memory_space=pl.ANY)
    num_tok, width = tok_rows.shape
    heads, dim = self_k.shape[3:]
    bf16, f32 = jnp.bfloat16, jnp.float32
    return pl.pallas_call(
        layers_kernel,
        out_shape=(jax.ShapeDtypeStruct((num_tok, width), bf16), jax.ShapeDtypeStruct(self_k.shape, bf16), jax.ShapeDtypeStruct(self_v.shape, bf16)),
        in_specs=[smem, smem] + [vmem] * 5 + [any_spec] * 7,
        out_specs=(vmem, any_spec, any_spec),
        scratch_shapes=[
            pltpu.VMEM(attn_full.shape[1:], bf16), pltpu.VMEM(fc1_full.shape[1:], bf16), pltpu.VMEM(fc2_full.shape[1:], bf16),
            pltpu.VMEM(self_k.shape, bf16), pltpu.VMEM(self_v.shape, bf16), pltpu.VMEM(cross_k.shape[1:], bf16), pltpu.VMEM(cross_v.shape[1:], bf16),
            pltpu.VMEM((num_tok, heads, dim), f32), pltpu.VMEM((num_tok, heads, dim), f32), pltpu.VMEM((num_tok, heads, dim), f32), pltpu.VMEM((num_tok, heads, dim), f32),
            pltpu.VMEM((num_tok, width), f32), pltpu.VMEM((num_tok, fc1_full.shape[2]), bf16),
            pltpu.SemaphoreType.DMA((8,)), pltpu.SemaphoreType.DMA((3, 2)), pltpu.SemaphoreType.DMA((2, 2)),
        ],
        compiler_params=pltpu.CompilerParams(vmem_limit_bytes=63 * 1024 * 1024),
        cost_estimate=pl.CostEstimate(flops=8_000_000_000, bytes_accessed=110_000_000, transcendentals=4_000_000),
        name='run_layers',
    )(positions, src_len, tok_rows, pos_rows, emb_norm, table, fc1_b, attn_full, fc1_full, fc2_full, self_k, self_v, cross_k, cross_v)


def logits_kernel(emb_ref, rows_ref, bias_ref, out_ref):
    steps, num_rows, _ = rows_ref.shape
    block = emb_ref.shape[0]
    lanes = 128
    stride = steps * num_rows // lanes
    for step in range(steps):
        scores = lax.dot_general(emb_ref[...], rows_ref[step], (((1,), (1,)), ((), ())), preferred_element_type=jnp.float32) + bias_ref[...]
        for part in range(num_rows // lanes):
            out_ref[pl.ds(part * steps + step, block, stride=stride), :] = scores[:, part * lanes:(part + 1) * lanes]


def run_logits(tok_embed, all_rows, bias):
    vocab, width = tok_embed.shape
    steps, num_rows, _ = all_rows.shape
    block = 400
    per = steps * num_rows // 128
    out = pl.pallas_call(
        logits_kernel,
        grid=(pl.cdiv(vocab, block),),
        out_shape=jax.ShapeDtypeStruct((vocab * per, 128), jnp.float32),
        in_specs=[pl.BlockSpec((block, width), lambda i: (i, 0)), pl.BlockSpec((steps, num_rows, width), lambda i: (0, 0, 0)), pl.BlockSpec((block, 1), lambda i: (i, 0))],
        out_specs=pl.BlockSpec((block * per, 128), lambda i: (i, 0)),
        compiler_params=pltpu.CompilerParams(dimension_semantics=('arbitrary',), vmem_limit_bytes=67_043_328),
        cost_estimate=pl.CostEstimate(flops=2 * vocab * width * steps * num_rows, bytes_accessed=20_000_000, transcendentals=0),
        name='run_logits',
    )(tok_embed, all_rows, bias[:, None])
    return out.reshape(vocab, num_rows // 128, steps, 128).transpose(2, 1, 3, 0).reshape(steps, num_rows, vocab)


def solution(mesh):
    cache_spec = P(None, 'fsdp')
    in_specs = (P('fsdp'), P('fsdp'), P('fsdp'), cache_spec, cache_spec, cache_spec, cache_spec,
                P(None, None, 'fsdp'), P(None, None, 'fsdp'), P(None, 'fsdp'), P(None, 'fsdp'),
                P(None, 'fsdp'), P(None, 'fsdp'), P(None, None, 'fsdp'), P(None, None, 'fsdp'),
                P('fsdp'), P(), P(), P('fsdp'))
    out_specs = (P(None, None, 'fsdp'), cache_spec, cache_spec)

    def local_decode(tokens, positions, src_len, self_k, self_v, cross_k, cross_v, attn_w, attn_b, fc1_w, fc1_b, fc2_w, fc2_b, ln_gain, ln_bias, tok_embed, pos_embed, emb_norm, logit_bias):
        shard_idx = lax.axis_index('fsdp')
        num_layers = attn_w.shape[0]
        num_rows, num_steps = tokens.shape
        vocab_local, width = tok_embed.shape
        num_dev = mesh.shape['fsdp']
        small = (attn_b, fc2_b, ln_gain, ln_bias, tokens.T, fc1_b)
        packed = jnp.concatenate([part.astype(jnp.float32).reshape(-1, num_rows) for part in small], axis=0)
        gathered, found, attn_full, fc1_full, fc2_full = gather_weights(packed, num_steps * num_rows, tok_embed, attn_w, fc1_w, fc2_w)
        table = gathered.transpose(1, 0, 2).reshape(packed.shape[0], num_dev * num_rows)
        all_fc1_b = gathered[:, ROW_FC1:].reshape(num_dev, num_layers, -1).transpose(1, 0, 2).reshape(num_layers, -1)
        all_tokens = gathered[:, ROW_TOKEN:ROW_TOKEN + num_steps].astype(jnp.int32).reshape(num_dev, num_steps * num_rows)
        owner = all_tokens // vocab_local
        most = (owner[:, :, None] == jnp.arange(num_dev)).astype(jnp.int32).sum(axis=1).max()
        my_owner = (tokens.T // vocab_local).reshape(-1)
        order = jnp.arange(num_steps * num_rows)
        my_rank = ((my_owner[None, :] == my_owner[:, None]) & (order[None, :] < order[:, None])).astype(jnp.int32).sum(axis=1)

        def few(found):
            line = my_owner * SLOTS + my_rank
            chosen = (line[:, None] == jnp.arange(num_dev * SLOTS)).astype(found.dtype)
            return jnp.dot(chosen, found.reshape(num_dev * SLOTS, width), preferred_element_type=jnp.float32).astype(found.dtype)

        def many(found):
            local = all_tokens - shard_idx * vocab_local
            mine = (local >= 0) & (local < vocab_local)
            rows = jnp.take(tok_embed, jnp.clip(local, 0, vocab_local - 1), axis=0)
            rows = jnp.where(mine[:, :, None], rows, jnp.zeros_like(rows))
            rows = lax.all_to_all(rows, 'fsdp', 0, 0)
            return rows.astype(jnp.float32).sum(axis=0).astype(found.dtype)

        tok_rows = lax.cond(most > SLOTS, many, few, found)
        step_pos = positions[None, :] + jnp.arange(num_steps)[:, None]
        pos_rows = jnp.take(pos_embed, step_pos + 2, axis=0).reshape(num_steps * num_rows, width)
        rows, cache_k, cache_v = run_layers(positions, src_len, tok_rows, pos_rows, emb_norm, table, all_fc1_b, attn_full, fc1_full, fc2_full, self_k, self_v, cross_k, cross_v)
        all_rows = gather_rows(rows.reshape(num_steps, num_rows, width))
        return run_logits(tok_embed, all_rows, logit_bias), cache_k, cache_v

    return jax.shard_map(local_decode, mesh=mesh, in_specs=in_specs, out_specs=out_specs, check_vma=False)
```

time: 956 us -> 379 us (0.40)
  blocking collectives: 398 us -> 0 us
  Pallas kernels: 0 us -> 359 us
  other arithmetic: 178 us -> 3.12 us
  matrix products: 147 us -> 0.34 us
  local copies, waits for them, and re-layouts: 122 us -> 14.1 us
  waiting for transfers between devices: 90 us -> 0 us
  between operations: 15.3 us -> 1.45 us
    all_gather x9 -> x0, blocking collectives: 360 us -> none  [the longest x2 80.5 us: local_decode(): ln_shifts = lax.all_gather(ln_bias[layer_idx], 'fsdp', axis=1, tiled=True)]
    pallas_call x0 -> x4, Pallas kernels: none -> 359 us  [the longest x1 252 us: gather_weights(): pl.pallas_call(weights_kernel, out_shape=(jax.ShapeDtypeStruct((NUM_DEV,)...]
    dot_general x38 -> x1, matrix products: 147 us -> 0.34 us  [few(): jnp.dot(chosen, found.reshape(num_dev * SLOTS, width), preferred_element_...]
    all_gather x8 -> x0, waiting for transfers between devices: 87.4 us -> none  [the longest x2 87.4 us: local_decode(): lax.all_gather(hidden.astype(jnp.bfloat16), 'fsdp', axis=0, tiled=True)]
    add x4 -> x1, other arithmetic: 48.1 us -> 0.01 us  [few(): line = my_owner * SLOTS + my_rank]
    unnamed x156 -> x13, local copies, waits for them, and re-layouts: 46.3 us -> 3.86 us
    unnamed x1 -> x0, blocking collectives: 38.8 us -> none
    select_n x5 -> x4, other arithmetic: 31.8 us -> 0.77 us  [the longest x2 0.75 us: local_decode(): jnp.take(pos_embed, step_pos + 2, axis=0)]
  transfers between devices with their start and end apart: 9 -> 0, of which waited for: 2 -> 0; matrix products, arithmetic and copies ran while one was open for 34% -> 0% of each run, Pallas kernels for 0% -> 0%
where the time goes in v2:
time: 379 us; the launch traced here: 378 us
  Pallas kernels  359 us (95%)
  local copies, waits for them, and re-layouts  14.1 us (4%)
    pallas_call x1, Pallas kernels, gather_weights(): pl.pallas_call(weights_kernel, out_shape=(jax.ShapeDtypeStruct((NUM_DEV,)...  252 us
    pallas_call x1, Pallas kernels, run_layers(): pl.pallas_call(layers_kernel, out_shape=(jax.ShapeDtypeStruct((num_tok, w...  62.7 us
    pallas_call x1, Pallas kernels, gather_rows(): pl.pallas_call(rows_kernel, out_shape=jax.ShapeDtypeStruct((steps, share...  29.8 us
    pallas_call x1, Pallas kernels, run_logits(): pl.pallas_call(logits_kernel, grid=(pl.cdiv(vocab, block),), out_shape=ja...  14.3 us

profile of v2, /device:TPU:0, one launch (start us, length us, event | category | flops | bytes accessed | tf_op | source)
XLA Modules:
  0.0 378.3 jit_solution(13823388789495201485)
XLA Ops:
  0.6 0.9 slice.25
  1.6 0.7 copy.64
  2.2 0.7 copy.65
  2.9 0.7 copy.66
  3.6 0.7 reshape.236
  4.4 0.7 convert_bitcast_fusion
  5.1 0.9 concatenate.5.small
  6.0 0.0 copy-start
  6.0 1.1 copy-done
  7.1 0.0 copy-start.1
  7.1 1.0 copy-done.1
  8.2 0.0 copy-start.2
  8.2 1.0 copy-done.2
  9.2 0.0 copy-start.4
  9.2 252.3 %gather_weights.1 = (f32[32,36,32]{2,1,0:T(8,128)S(1)}, bf16[32,16,1024]{2,1,0:T(8,128)(2,1)S(1)}, bf16[2,6,1024,1024]{3,2,1,0:T(8,128)(2,1)}, bf16[2,1024,4096]{2,1,0:T(8,128)(2,1)}, bf16[2,4096,1024]{2,1,0:T(8,128)(2,1)}) custom-call(f32[36,32]{1,0:T(8,128)S(1)} %concatenate.5.small, bf16[128,1024]{1,0:T(8,128)(2,1)S(1)} %scatter.4.tail, ...), custom_call_target="tpu_custom_call" | custom-call | flops 199999995904 | bytes 120000000 | tf_op jit(solution)/shard_map/gather_weights/pallas_call | solution.py:282
  261.5 0.1 broadcast_divide_fusion
  261.6 0.1 copy.76
  261.7 0.1 compare_and_fusion.2
  261.8 0.1 copy.67
  261.9 0.1 copy.70
  261.9 0.6 convert_reduce_fusion
  262.6 0.6 reduce_max.9
  263.9 0.0 copy-done.4
  263.9 0.1 reshape.222
  264.0 0.1 fusion.2
  264.1 0.0 copy-start.5
  264.1 0.7 conditional.1
  264.1 0.1 reduce_sum.28
  264.2 0.3 convolution_convert_fusion
  264.8 0.1 copy.72
  264.9 1.0 reshape.223.table_ref
  265.9 0.1 reshape.224
  266.0 0.6 copy.80
  266.6 0.0 copy-done.5
  266.6 0.1 add.111
  266.7 0.1 add.114
  266.8 0.1 reshape.247
  266.9 2.7 gather_fusion.1
  269.6 0.7 broadcast_select_fusion.posrow_ref
  270.3 62.7 %run_layers.1 = (bf16[64,1024]{1,0:T(8,128)(2,1)}, bf16[2,32,32,16,64]{4,3,2,1,0:T(8,128)(2,1)}, bf16[2,32,32,16,64]{4,3,2,1,0:T(8,128)(2,1)}) custom-call(s32[32]{0:T(128)} %pos_ref.1, s32[32]{0:T(128)} %len_ref.1, bf16[64,1024]{1,0:T(8,128)(2,1)S(1)} %get-tuple-element.66.tok_ref, bf16[64,1024]{1,0:T(8,128)(2,1)} %broadcast_select_fusion.posrow_ref, ...), custom_call_target="tpu_custom_call" | custom-call | flops 8000000000 | bytes 110000000 | tf_op jit(solution)/shard_map/run_layers/pallas_call | solution.py:519
  333.0 0.0 copy-start.3
  333.0 29.8 %gather_rows.1.rows_ref = bf16[2,1024,1024]{2,1,0:T(8,128)(2,1)} custom-call(bf16[2,32,1024]{2,1,0:T(8,128)(2,1)} %bitcast.44), custom_call_target="tpu_custom_call" | custom-call | flops 20000000000 | bytes 8000000 | tf_op jit(solution)/shard_map/gather_rows/pallas_call | solution.py:319
  362.8 0.0 copy-done.3
  362.8 1.2 broadcast_in_dim.44.bias_ref
  364.0 14.3 %run_logits.1 = f32[25152,128]{1,0:T(8,128)} custom-call(bf16[1572,1024]{1,0:T(8,128)(2,1)} %emb_ref.1, bf16[2,1024,1024]{2,1,0:T(8,128)(2,1)} %gather_rows.1.rows_ref, f32[1572,1]{1,0:T(8,128)} %broadcast_in_dim.44.bias_ref), custom_call_target="tpu_custom_call" | custom-call | flops 6593445888 | bytes 20000000 | tf_op jit(solution)/shard_map/run_logits/pallas_call | solution.py:553
  (14 shorter events, 0.2 us)
Async XLA Ops:
  6.0 1.1 copy-start
  7.1 1.0 copy-start.1
  8.2 1.0 copy-start.2
  9.2 254.7 %copy-start.4 = (s32[32,2]{0,1:T(2,128)S(1)}, s32[32,2]{0,1:T(2,128)}, u32[]{:S(2)}) copy-start(s32[32,2]{0,1:T(2,128)} %param.23) | copy-start | bytes 772
  264.1 2.5 copy-start.5
  333.0 29.8 %copy-start.3 = (f32[1572]{0:T(1024)S(1)}, f32[1572]{0:T(1024)}, u32[]{:S(2)}) copy-start(f32[1572]{0:T(1024)} %param.41) | copy-start | bytes 18868

commit v3 on v2

--- a/solution.py
+++ b/solution.py
@@ -548,7 +548,7 @@
 def run_logits(tok_embed, all_rows, bias):
     vocab, width = tok_embed.shape
     steps, num_rows, _ = all_rows.shape
-    block = 400
+    block = 528
     per = steps * num_rows // 128
     out = pl.pallas_call(
         logits_kernel,

time: 379 us -> 379 us (level)
  no operation moved by 1% of the time
where the time goes in v3:
time: 379 us; the launch traced here: 378 us
  Pallas kernels  359 us (95%)
  local copies, waits for them, and re-layouts  14.1 us (4%)
    pallas_call x1, Pallas kernels, gather_weights(): pl.pallas_call(weights_kernel, out_shape=(jax.ShapeDtypeStruct((NUM_DEV,)...  252 us
    pallas_call x1, Pallas kernels, run_layers(): pl.pallas_call(layers_kernel, out_shape=(jax.ShapeDtypeStruct((num_tok, w...  62.7 us
    pallas_call x1, Pallas kernels, gather_rows(): pl.pallas_call(rows_kernel, out_shape=jax.ShapeDtypeStruct((steps, share...  29.8 us
    pallas_call x1, Pallas kernels, run_logits(): pl.pallas_call(logits_kernel, grid=(pl.cdiv(vocab, block),), out_shape=ja...  14.4 us

profile of v3, /device:TPU:0, one launch (start us, length us, event | category | flops | bytes accessed | tf_op | source)
XLA Modules:
  0.0 378.4 jit_solution(16033782015196490170)
XLA Ops:
  0.6 0.9 slice.25
  1.6 0.7 copy.64
  2.2 0.7 copy.65
  2.9 0.7 copy.66
  3.6 0.7 reshape.236
  4.4 0.7 convert_bitcast_fusion
  5.1 0.9 concatenate.5.small
  6.0 0.0 copy-start
  6.0 1.1 copy-done
  7.1 0.0 copy-start.1
  7.1 1.0 copy-done.1
  8.2 0.0 copy-start.2
  8.2 1.0 copy-done.2
  9.2 0.0 copy-start.4
  9.2 252.3 %gather_weights.1 = (f32[32,36,32]{2,1,0:T(8,128)S(1)}, bf16[32,16,1024]{2,1,0:T(8,128)(2,1)S(1)}, bf16[2,6,1024,1024]{3,2,1,0:T(8,128)(2,1)}, bf16[2,1024,4096]{2,1,0:T(8,128)(2,1)}, bf16[2,4096,1024]{2,1,0:T(8,128)(2,1)}) custom-call(f32[36,32]{1,0:T(8,128)S(1)} %concatenate.5.small, bf16[128,1024]{1,0:T(8,128)(2,1)S(1)} %scatter.4.tail, ...), custom_call_target="tpu_custom_call" | custom-call | flops 199999995904 | bytes 120000000 | tf_op jit(solution)/shard_map/gather_weights/pallas_call | solution.py:282
  261.5 0.1 broadcast_divide_fusion
  261.6 0.1 copy.76
  261.7 0.1 compare_and_fusion.2
  261.8 0.1 copy.67
  261.9 0.1 copy.70
  261.9 0.6 convert_reduce_fusion
  262.6 0.6 reduce_max.9
  263.9 0.0 copy-done.4
  263.9 0.1 reshape.222
  264.0 0.1 fusion.2
  264.1 0.0 copy-start.5
  264.1 0.7 conditional.1
  264.1 0.1 reduce_sum.28
  264.2 0.3 convolution_convert_fusion
  264.8 0.1 copy.72
  264.9 1.0 reshape.223.table_ref
  265.9 0.1 reshape.224
  266.0 0.6 copy.80
  266.6 0.0 copy-done.5
  266.6 0.1 add.111
  266.7 0.1 add.114
  266.8 0.1 reshape.247
  266.9 2.7 gather_fusion.1
  269.6 0.7 broadcast_select_fusion.posrow_ref
  270.3 62.7 %run_layers.1 = (bf16[64,1024]{1,0:T(8,128)(2,1)}, bf16[2,32,32,16,64]{4,3,2,1,0:T(8,128)(2,1)}, bf16[2,32,32,16,64]{4,3,2,1,0:T(8,128)(2,1)}) custom-call(s32[32]{0:T(128)} %pos_ref.1, s32[32]{0:T(128)} %len_ref.1, bf16[64,1024]{1,0:T(8,128)(2,1)S(1)} %get-tuple-element.66.tok_ref, bf16[64,1024]{1,0:T(8,128)(2,1)} %broadcast_select_fusion.posrow_ref, ...), custom_call_target="tpu_custom_call" | custom-call | flops 8000000000 | bytes 110000000 | tf_op jit(solution)/shard_map/run_layers/pallas_call | solution.py:519
  333.0 0.0 copy-start.3
  333.0 29.8 %gather_rows.1.rows_ref = bf16[2,1024,1024]{2,1,0:T(8,128)(2,1)} custom-call(bf16[2,32,1024]{2,1,0:T(8,128)(2,1)} %bitcast.44), custom_call_target="tpu_custom_call" | custom-call | flops 20000000000 | bytes 8000000 | tf_op jit(solution)/shard_map/gather_rows/pallas_call | solution.py:319
  362.8 0.0 copy-done.3
  362.8 1.2 broadcast_in_dim.44.bias_ref
  364.0 14.4 %run_logits.1 = f32[25152,128]{1,0:T(8,128)} custom-call(bf16[1572,1024]{1,0:T(8,128)(2,1)} %emb_ref.1, bf16[2,1024,1024]{2,1,0:T(8,128)(2,1)} %gather_rows.1.rows_ref, f32[1572,1]{1,0:T(8,128)} %broadcast_in_dim.44.bias_ref), custom_call_target="tpu_custom_call" | custom-call | flops 6593445888 | bytes 20000000 | tf_op jit(solution)/shard_map/run_logits/pallas_call | solution.py:553
  (14 shorter events, 0.2 us)
Async XLA Ops:
  6.0 1.1 copy-start
  7.1 1.0 copy-start.1
  8.2 1.0 copy-start.2
  9.2 254.7 %copy-start.4 = (s32[32,2]{0,1:T(2,128)S(1)}, s32[32,2]{0,1:T(2,128)}, u32[]{:S(2)}) copy-start(s32[32,2]{0,1:T(2,128)} %param.23) | copy-start | bytes 772
  264.1 2.5 copy-start.5
  333.0 29.8 %copy-start.3 = (f32[1572]{0:T(1024)S(1)}, f32[1572]{0:T(1024)}, u32[]{:S(2)}) copy-start(f32[1572]{0:T(1024)} %param.41) | copy-start | bytes 18868
